TPU v7x, 128 devices: a whole 4x4x4 slice. The times are simulated.
128 devices in a mesh: win: 8 (over z, core), step: 16 (over x, y).
Axes of the slice: x: 4, y: 4, z: 4, core: 2. Of those that a mesh axis runs over, the one named last changes fastest.
Arguments:
- initial_state: float32 [32, 32, 128], replicated, may hold values from -6 to 6
- source: float32 [8, 16, 32, 32, 128], P('win', 'step'), may hold values from -6 to 6
- absorption: float32 [32, 32, 128], replicated, may hold values from 0.01 to 0.2
Outputs:
- state: float32 [8, 16, 32, 32, 128], P('win', 'step')
All inputs are finite; a program needn't handle non-finite values.
Results may differ from a plain program's by a relative error of at most 0.00026.
Values sent between devices are 32-bit elements; how exact they have to be, the bound alone decides.
A program may use at most 64 MiB of HBM per device.

v0:
```python
import math

import jax
import jax.numpy as jnp
from jax import lax
from jax.sharding import PartitionSpec as P

ITERS = 2
SWEEPS = 8


alpha_corner = 0.1
coupling = 0.05


def side_by_side(arrays, axis, split_dim, concat_dim, along):
    ends, at = ([], 0)
    for a in arrays[:-1]:
        at += a.shape[along]
        ends.append(at)
    both = jnp.concatenate(arrays, axis=along)
    return tuple(
        jnp.split(
            lax.all_to_all(both, axis, split_axis=split_dim, concat_axis=concat_dim, tiled=True),
            ends,
            axis=along,
        )
    )


def from_behind(block, axis, distance):
    devices = range(lax.axis_size(axis))
    route = [(i - distance, i) for i in devices if i - distance in devices]
    return lax.ppermute(block, axis, route)


def pad_cube(field):
    widths = [(0, 0)] * (field.ndim - 3) + [(1, 1)] * 3
    return jnp.pad(field, widths)


def neighbours(field):
    padded = pad_cube(field)
    total = padded[..., 2:, 1:-1, 1:-1] + padded[..., :-2, 1:-1, 1:-1]
    total = total + padded[..., 1:-1, 2:, 1:-1] + padded[..., 1:-1, :-2, 1:-1]
    total = total + padded[..., 1:-1, 1:-1, 2:] + padded[..., 1:-1, 1:-1, :-2]
    return total


def complex_times(first, second):
    return jnp.stack(
        [first[0] * second[0] - first[1] * second[1], first[0] * second[1] + first[1] * second[0]]
    )


def relax(spectrum, inverse):
    field = complex_times(inverse, spectrum)
    for repeat in range(SWEEPS - 1):
        field = complex_times(inverse, spectrum + coupling * neighbours(field))
    return field


def inverse_diagonal(angle, absorption, gamma):
    real_part = 1.0 - gamma * jnp.cos(angle) + absorption + 6.0 * coupling
    imag_part = jnp.broadcast_to(gamma * jnp.sin(angle), real_part.shape)
    magnitude = real_part * real_part + imag_part * imag_part
    return jnp.stack([real_part / magnitude, -imag_part / magnitude])


def dft_tables(window_len):
    index = jnp.arange(window_len, dtype=jnp.int32)
    product = index[:, None] * index[None, :] % window_len
    angle = product.astype(jnp.float32) * (2.0 * math.pi / window_len)
    return (jnp.cos(angle), jnp.sin(angle))


def transform_exchange(scaled, window_len):
    pencil = lax.all_to_all(scaled[None], "step", split_axis=1, concat_axis=0, tiled=True)
    cosine, sine = dft_tables(window_len)
    flat = pencil.reshape(window_len, -1)
    real_part = jnp.dot(cosine, flat, precision=lax.Precision.HIGHEST)
    imag_part = -jnp.dot(sine, flat, precision=lax.Precision.HIGHEST)
    shaped = pencil.shape
    spectrum = side_by_side((real_part.reshape(shaped), imag_part.reshape(shaped)), "step", 0, 1, 2)
    return jnp.stack([spectrum[0][0], spectrum[1][0]])


def untransform_exchange(field, window_len):
    pencil = side_by_side((field[0][None], field[1][None]), "step", 1, 0, 2)
    cosine, sine = dft_tables(window_len)
    shaped = pencil[0].shape
    values = jnp.dot(cosine, pencil[0].reshape(window_len, -1), precision=lax.Precision.HIGHEST)
    values = values - jnp.dot(
        sine, pencil[1].reshape(window_len, -1), precision=lax.Precision.HIGHEST
    )
    values = values / window_len
    result = lax.all_to_all(values.reshape(shaped), "step", split_axis=0, concat_axis=1, tiled=True)
    return result[0]


def per_device(initial_state, source, absorption):
    window_len = lax.axis_size("step")
    moment = lax.axis_index("step")
    window_index = lax.axis_index("win")
    gamma = alpha_corner ** (1.0 / window_len)
    scale = gamma ** moment.astype(jnp.float32)
    forcing_base = source[0, 0]
    is_first = moment == 0
    state = jnp.zeros_like(forcing_base)
    angle = moment.astype(jnp.float32) * (2.0 * math.pi / window_len)
    inverse = inverse_diagonal(angle, absorption, gamma)
    for repeat in range(ITERS):
        if repeat == 0:
            correction = jnp.where(window_index == 0, initial_state, 0.0)
        else:
            ends = from_behind(state, "step", 1 - window_len)
            before = from_behind(ends, "win", 1)
            before = jnp.where(window_index == 0, initial_state, before)
            correction = before - alpha_corner * ends
        forcing = forcing_base + jnp.where(is_first, correction, 0.0)
        scaled = forcing * scale
        spectrum = transform_exchange(scaled, window_len)
        field = relax(spectrum, inverse)
        values = untransform_exchange(field, window_len)
        state = values / scale
    return state[None, None]


def solution(mesh):
    return jax.shard_map(
        per_device,
        mesh=mesh,
        in_specs=(P(), P("win", "step", None, None, None), P()),
        out_specs=P("win", "step", None, None, None),
        check_vma=False,
    )
```

profile of v0, /device:TPU:32, one launch (start us, length us, event | category | flops | bytes accessed | tf_op | source)
XLA Modules:
  0.0 208.4 jit_solution(9015983651513409568)
XLA Ops:
  0.0 1.2 fusion.58
  1.2 18.3 %all_to_all.84 = f32[1,32,32,128]{3,2,0,1:T(8,128)S(1)} all-to-all(f32[1,32,32,128]{3,2,0,1:T(8,128)S(1)} %fusion.58), channel_id=1, replica_groups=mesh['win'=8,'step'=16] {'step'}, dimensions={1} | all-to-all | bytes 1048576 | tf_op jit(solution)/shard_map/all_to_all | solution.py:78
  20.4 0.9 fusion.63
  21.7 1.3 copy.12
  23.1 3.8 %all-to-all-start.1 = ((f32[16,2,64,128]{3,2,1,0:T(8,128)}), f32[16,2,64,128]{3,2,1,0:T(8,128)S(1)}, u32[]{:S(2)}, u32[]{:S(2)}) async-start(f32[16,2,64,128]{3,2,1,0:T(8,128)} %copy.12), calls=%async_computation.1 | async-start | bytes 2097152 | tf_op jit(solution)/shard_map/all_to_all | solution.py:24
  27.1 15.6 %all-to-all-done.1 = f32[16,2,64,128]{3,2,1,0:T(8,128)S(1)} async-done(((f32[16,2,64,128]{3,2,1,0:T(8,128)}), f32[16,2,64,128]{3,2,1,0:T(8,128)S(1)}, u32[]{:S(2)}, u32[]{:S(2)}) %all-to-all-start.1) | async-done | bytes 1048608 | tf_op jit(solution)/shard_map/all_to_all | solution.py:24
  43.8 1.4 fusion.38
  46.2 1.4 fusion.36
  48.7 1.4 fusion.34
  51.1 1.4 fusion.32
  53.5 1.6 fusion.30
  56.2 1.4 fusion.28
  58.6 1.4 fusion.26
  60.4 19.1 %all_to_all.85 = f32[1,32,64,128]{3,2,0,1:T(8,128)S(1)} all-to-all(f32[1,32,64,128]{3,2,0,1:T(8,128)S(1)} %maximum_bitcast_fusion), channel_id=1, replica_groups=mesh['win'=8,'step'=16] {'step'}, dimensions={1} | all-to-all | bytes 2097152 | tf_op jit(solution)/shard_map/all_to_all | solution.py:24
  80.4 0.9 fusion.8
  81.4 13.4 %all_to_all.86 = f32[16,2,32,128]{3,2,1,0:T(8,128)S(1)} all-to-all(f32[16,2,32,128]{3,2,1,0:T(8,128)S(1)} %bitcast.372), channel_id=1, replica_groups=mesh['win'=8,'step'=16] {'step'}, dimensions={0} | all-to-all | bytes 1048576 | tf_op jit(solution)/shard_map/all_to_all | solution.py:97
  94.9 1.3 collective-permute-start
  96.2 13.6 %collective-permute-done = f32[32,32,128]{2,1,0:T(8,128)S(1)} collective-permute-done((f32[32,32,128]{2,1,0:T(8,128)S(1)}, f32[32,32,128]{2,1,0:T(8,128)S(1)}, u32[]{:S(2)}, u32[]{:S(2)}) %collective-permute-start) | collective-permute-done | bytes 524320 | tf_op jit(solution)/shard_map/ppermute | solution.py:34
  109.7 1.9 collective-permute-start.1
  111.7 8.6 %collective-permute-done.1 = f32[32,32,128]{2,1,0:T(8,128)S(1)} collective-permute-done((f32[32,32,128]{2,1,0:T(8,128)S(1)}, f32[32,32,128]{2,1,0:T(8,128)S(1)}, u32[]{:S(2)}, u32[]{:S(2)}) %collective-permute-start.1) | collective-permute-done | bytes 524320 | tf_op jit(solution)/shard_map/ppermute | solution.py:34
  120.5 14.1 %all_to_all.87 = f32[1,32,32,128]{3,2,0,1:T(8,128)S(1)} all-to-all(f32[1,32,32,128]{3,2,0,1:T(8,128)S(1)} %fusion.60), channel_id=1, replica_groups=mesh['win'=8,'step'=16] {'step'}, dimensions={1} | all-to-all | bytes 1048576 | tf_op jit(solution)/shard_map/all_to_all | solution.py:78
  137.1 19.3 %all_to_all.88 = f32[16,2,64,128]{3,2,1,0:T(8,128)S(1)} all-to-all(f32[16,2,64,128]{3,2,1,0:T(8,128)S(1)} %copy.17), channel_id=1, replica_groups=mesh['win'=8,'step'=16] {'step'}, dimensions={0} | all-to-all | bytes 2097152 | tf_op jit(solution)/shard_map/all_to_all | solution.py:24
  157.5 1.4 fusion.24
  159.9 1.4 fusion.22
  162.3 1.4 fusion.20
  164.8 1.4 fusion.18
  167.2 1.6 fusion.16
  169.8 1.4 fusion.14
  172.3 1.4 fusion.12
  174.0 18.0 %all_to_all.89 = f32[1,32,64,128]{3,2,0,1:T(8,128)S(1)} all-to-all(f32[1,32,64,128]{3,2,0,1:T(8,128)S(1)} %maximum_bitcast_fusion.1), channel_id=1, replica_groups=mesh['win'=8,'step'=16] {'step'}, dimensions={1} | all-to-all | bytes 2097152 | tf_op jit(solution)/shard_map/all_to_all | solution.py:24
  194.0 13.3 %all_to_all.90 = f32[16,2,32,128]{3,2,1,0:T(8,128)S(1)} all-to-all(f32[16,2,32,128]{3,2,1,0:T(8,128)S(1)} %bitcast.375), channel_id=1, replica_groups=mesh['win'=8,'step'=16] {'step'}, dimensions={0} | all-to-all | bytes 1048576 | tf_op jit(solution)/shard_map/all_to_all | solution.py:97
  207.3 0.9 broadcast_divide_fusion
  (63 shorter events, 21.7 us)
Async XLA Ops:
  21.7 21.0 %copy-start = (f32[32,32,128]{2,1,0:T(8,128)S(1)}, f32[32,32,128]{2,1,0:T(8,128)}, u32[]{:S(2)}) copy-start(f32[32,32,128]{2,1,0:T(8,128)} %param.5) | copy-start | bytes 1572868
  23.1 19.6 %all-to-all-start.1 = ((f32[16,2,64,128]{3,2,1,0:T(8,128)}), f32[16,2,64,128]{3,2,1,0:T(8,128)S(1)}, u32[]{:S(2)}, u32[]{:S(2)}) async-start(f32[16,2,64,128]{3,2,1,0:T(8,128)} %copy.12), calls=%async_computation.1 | async-start | bytes 2097152 | tf_op jit(solution)/shard_map/all_to_all | solution.py:24
  79.5 40.7 %copy-start.1 = (f32[1,1,32,32,128]{4,3,2,1,0:T(8,128)S(1)}, f32[1,1,32,32,128]{4,3,2,1,0:T(8,128)}, u32[]{:S(2)}) copy-start(f32[1,1,32,32,128]{4,3,2,1,0:T(8,128)} %param.4) | copy-start | bytes 1572868
  79.5 40.7 %copy-start.2 = (f32[32,32,128]{2,1,0:T(8,128)S(1)}, f32[32,32,128]{2,1,0:T(8,128)}, u32[]{:S(2)}) copy-start(f32[32,32,128]{2,1,0:T(8,128)} %param.3) | copy-start | bytes 1572868
  94.9 14.9 %collective-permute-start = (f32[32,32,128]{2,1,0:T(8,128)S(1)}, f32[32,32,128]{2,1,0:T(8,128)S(1)}, u32[]{:S(2)}, u32[]{:S(2)}) collective-permute-start(f32[32,32,128]{2,1,0:T(8,128)S(1)} %bitcast.378), channel_id=1, source_target_pairs={{15,0},{31,16},{47,32},{63,48},{79,64},{95,80},{111,96},{127,112}} | collective-permute-start | bytes 1572872 | tf_op jit(solution)/shard_map/ppermute | solution.py:34
  109.7 10.5 %collective-permute-start.1 = (f32[32,32,128]{2,1,0:T(8,128)S(1)}, f32[32,32,128]{2,1,0:T(8,128)S(1)}, u32[]{:S(2)}, u32[]{:S(2)}) collective-permute-start(f32[32,32,128]{2,1,0:T(8,128)S(1)} %collective-permute-done), channel_id=1, source_target_pairs={{0,16},{16,32},{32,48},{48,64},{64,80},{80,96},{96,112},{1,17},{17... | collective-permute-start | bytes 1572872 | tf_op jit(solution)/shard_map/ppermute | solution.py:34
where the time goes:
time: 212 us; the launch traced here: 208 us
  blocking collectives  116 us (55%)
  waiting for transfers between devices  37.8 us (18%)
  other arithmetic  37.3 us (18%)
  starting transfers between devices  7.03 us (3%)
  matrix products  6.33 us (3%)
  local copies, waits for them, and re-layouts  3.44 us (2%)
    all_to_all x3, blocking collectives, side_by_side(): lax.all_to_all(both, axis, split_axis=split_dim, concat_axis=concat_dim,...  56.3 us
    all_to_all x2, blocking collectives, transform_exchange(): lax.all_to_all(scaled[None], 'step', split_axis=1, concat_axis=0, tiled=T...  32.4 us
    all_to_all x2, blocking collectives, untransform_exchange(): lax.all_to_all(values.reshape(shaped), 'step', split_axis=0, concat_axis=...  26.8 us
    ppermute x2, waiting for transfers between devices, from_behind(): return lax.ppermute(block, axis, route)  22.1 us
    add x14, other arithmetic, relax(): field = complex_times(inverse, spectrum + coupling * neighbours(field))  20.3 us
    all_to_all x1, waiting for transfers between devices, side_by_side(): lax.all_to_all(both, axis, split_axis=split_dim, concat_axis=concat_dim,...  15.6 us
    another operation x30, other arithmetic, complex_times(): jnp.stack([first[0] * second[0] - first[1] * second[1], first[0] * second...  14.4 us
  transfers between devices with their start and end apart: 3, of which 3 were waited for; matrix products, arithmetic and copies ran while one was open for 0% of the time, Pallas kernels for 0%

commit v1 on v0

v1 whole, which is shorter than its diff:
```python
import functools
import math

import jax
import jax.numpy as jnp
from jax import lax
from jax.experimental import pallas as pl
from jax.experimental.pallas import tpu as pltpu
from jax.sharding import PartitionSpec as P

SWEEPS = 8
STEPS = 16
WINDOWS = 8
SLOTS = 8
ALPHA = 0.1
COUPLING = 0.05
GAMMA = ALPHA ** (1.0 / STEPS)
NX, NY, NZ = 32, 32, 128
B = 8
MESH = pl.DeviceIdType.MESH
F32 = jnp.float32


def wpow(n, k):
    angle = 2.0 * math.pi * k / n
    return math.cos(angle), -math.sin(angle)


def times(c, s, re, im):
    if abs(s) < 1e-12:
        return (re, im) if c > 0 else (-re, None if im is None else -im)
    if abs(c) < 1e-12:
        if im is None:
            return None, (re if s > 0 else -re)
        return (-im, re) if s > 0 else (im, -re)
    if im is None:
        return c * re, s * re
    if abs(abs(c) - abs(s)) < 1e-12:
        h = abs(c)
        a, b = (re if c > 0 else -re), (im if c > 0 else -im)
        if c * s > 0:
            return h * (a - b), h * (b + a)
        return h * (a + b), h * (b - a)
    return c * re - s * im, c * im + s * re


def plus(a, b):
    return b if a is None else a if b is None else a + b


def minus(a, b):
    if b is None:
        return a
    return -b if a is None else a - b


def rdft(values):
    n = len(values)
    if n == 1:
        return [(values[0], None)]
    half = n // 2
    even, odd = rdft(values[0::2]), rdft(values[1::2])
    out = []
    for k in range(half + 1):
        if k == half:
            out.append((even[0][0] - odd[0][0], None))
            break
        if k <= half // 2:
            e, o = even[k], odd[k]
        else:
            e, o = even[half - k], odd[half - k]
            e = (e[0], None if e[1] is None else -e[1])
            o = (o[0], None if o[1] is None else -o[1])
        o = times(*wpow(n, k), *o)
        out.append((plus(e[0], o[0]), plus(e[1], o[1])))
    return out


def irdft(spectrum, n):
    if n == 1:
        return [spectrum[0][0]]
    half = n // 2
    even, odd = [], []
    for k in range(half // 2 + 1):
        x = spectrum[k]
        y = spectrum[half - k]
        ym = None if y[1] is None else -y[1]
        e = (plus(x[0], y[0]), plus(x[1], ym))
        d = (minus(x[0], y[0]), minus(x[1], ym))
        c, s = wpow(n, k)
        if 2 * k == half and half > 1:
            e = (x[0] + x[0], None)
            d = (None, x[1] + x[1])
        o = d if k == 0 else times_any(c, -s, *d)
        if k == 0 or 2 * k == half:
            e, o = (e[0], None), (o[0], None)
        even.append(e)
        odd.append(o)
    if half == 1:
        even, odd = even[:1], odd[:1]
    a, b = irdft(even, half), irdft(odd, half)
    out = [None] * n
    out[0::2], out[1::2] = a, b
    return out


def times_any(c, s, re, im):
    if re is None:
        r, i = times(c, s, im, None)
        return (None if i is None else -i), r
    return times(c, s, re, im)


def table(values, index):
    out = jnp.float32(values[0])
    for k in range(1, len(values)):
        out = jnp.where(index == k, jnp.float32(values[k]), out)
    return out


def kernel(
    src_hbm, init_hbm, abs_hbm, out_ref,
    src, ab, init, tbuf, sbuf, spec, kc, uu, ee, epart, ends, before, dext, kx, vv, f1, obuf,
    lsem, t1s, t1r, t2s, t2r, rss, rsr, wns, wnr, has, har, t3s, t3r, t4s, t4r,
):
    s = lax.axis_index("step")
    w = lax.axis_index("win")
    bx, by = s // 4, s % 4
    core = w % 2
    x0 = pl.multiple_of(bx * B, B)
    y0 = pl.multiple_of(by * B, B)
    slot = s // 2
    active = (bx + by + core) % 2 == 0

    def slot_device(f):
        return 2 * f + (f // 2 + core) % 2

    def origin(d):
        return pl.multiple_of((d // 4) * B, B), pl.multiple_of((d % 4) * B, B)

    def remote(source, target, send, recv, step=None, win=None):
        return pltpu.make_async_remote_copy(
            source, target, send, recv,
            device_id={"step": s if step is None else step, "win": w if win is None else win},
            device_id_type=MESH,
        )

    load_src = pltpu.make_async_copy(src_hbm, src, lsem.at[0])
    load_abs = pltpu.make_async_copy(abs_hbm, ab, lsem.at[1])
    load_init = pltpu.make_async_copy(init_hbm.at[pl.ds(x0, B), pl.ds(y0, B)], init, lsem.at[2])
    load_src.start()
    load_abs.start()
    load_init.start()

    barrier = pltpu.get_barrier_semaphore()
    for k in range(1, STEPS):
        pl.semaphore_signal(barrier, inc=1, device_id={"step": (s + k) % STEPS, "win": w}, device_id_type=MESH)
    for k in (1, WINDOWS - 1):
        pl.semaphore_signal(barrier, inc=1, device_id={"step": s, "win": (w + k) % WINDOWS}, device_id_type=MESH)
    pl.semaphore_wait(barrier, STEPS - 1 + 2)
    load_src.wait()

    t1 = []
    for k in range(1, STEPS):
        d = (s + k) % STEPS
        dx, dy = origin(d)
        copy = remote(src.at[pl.ds(dx, B), pl.ds(dy, B)], tbuf.at[s], t1s.at[k], t1r.at[s], step=d)
        copy.start()
        t1.append(copy)
    load_init.wait()
    load_abs.wait()
    tbuf[s] = src[pl.ds(x0, B), pl.ds(y0, B), :]

    cos_of = [math.cos(2 * math.pi * f / STEPS) for f in range(SLOTS)]
    sin_of = [math.sin(2 * math.pi * f / STEPS) for f in range(SLOTS)]
    c1 = table(cos_of, slot)
    c2 = table([-1.0] + cos_of[1:], slot)
    sn = table([0.0] + sin_of[1:], slot)

    def coefficients(a, cos1, cos2, sin):
        base = a + (1.0 + 6.0 * COUPLING)
        r1 = base - GAMMA * cos1
        im = GAMMA * sin
        scale1 = COUPLING / (r1 * r1 + im * im)
        r2 = base - GAMMA * cos2
        scale2 = COUPLING / (r2 * r2 + im * im)
        return r1 * scale1, r2 * scale2, -im * scale1

    @pl.when(active)
    def _():
        def plane(x, c):
            k1, k2, kb = coefficients(ab[x], c1, c2, sn)
            kc[0, x], kc[1, x], kc[2, x] = k1, k2, kb
            return c

        lax.fori_loop(0, NX, plane, 0, unroll=4)
        zero = jnp.zeros((48, NZ), F32)
        zrow = jnp.zeros((8, NZ), F32)
        for p in range(2):
            for c in range(2):
                uu[p, c, 0] = zero
                uu[p, c, NX + 1] = zero

        def rows(x, c):
            for p in range(2):
                for q in range(2):
                    uu[p, q, x, pl.ds(0, 8), :] = zrow
                    uu[p, q, x, pl.ds(40, 8), :] = zrow
            return c

        lax.fori_loop(1, NX + 1, rows, 0, unroll=4)

    def wide_plane(i, c):
        gx = x0 - B + i
        inx = jnp.logical_and(gx >= 0, gx < NX)
        gxc = jnp.clip(gx, 0, NX - 1)
        for b in range(3):
            gy = by - 1 + b
            inside = jnp.logical_and(inx, jnp.logical_and(gy >= 0, gy < 4))
            keep = jnp.where(inside, jnp.float32(1.0), jnp.float32(0.0))
            a = ab[gxc, pl.ds(pl.multiple_of(jnp.clip(gy, 0, 3) * B, B), B), :]
            for f in range(SLOTS):
                if f == 0:
                    first = keep * COUPLING / (a + (1.0 + 6.0 * COUPLING - GAMMA))
                    second = keep * COUPLING / (a + (1.0 + 6.0 * COUPLING + GAMMA))
                else:
                    r = a + (1.0 + 6.0 * COUPLING - GAMMA * cos_of[f])
                    im = GAMMA * sin_of[f]
                    scale = keep * COUPLING / (r * r + im * im)
                    first, second = r * scale, -im * scale
                kx[f, 0, i, pl.ds(b * B, B), :] = first
                kx[f, 1, i, pl.ds(b * B, B), :] = second
        return c

    lax.fori_loop(0, 3 * B, wide_plane, 0)

    for k in range(1, STEPS):
        d = (s - k) % STEPS
        remote(src.at[pl.ds(0, B), pl.ds(0, B)], tbuf.at[d], t1s.at[k], t1r.at[d], step=d).wait_recv()
    first_window = jnp.where(w == 0, jnp.float32(1.0), jnp.float32(0.0))

    def transform(x, c):
        values = []
        for t in range(STEPS):
            v = tbuf[t, x]
            if t == 0:
                v = v + first_window * init[x]
            values.append(v * (GAMMA**t / COUPLING))
        out = rdft(values)
        sbuf[0, 0, x], sbuf[0, 1, x] = out[0][0], out[8][0]
        for f in range(1, SLOTS):
            sbuf[f, 0, x], sbuf[f, 1, x] = out[f]
        return c

    lax.fori_loop(0, B, transform, 0)

    t2 = []
    for k in range(1, SLOTS):
        f = (slot + k) % SLOTS
        copy = remote(
            sbuf.at[f], spec.at[:, pl.ds(x0, B), pl.ds(y0, B)], t2s.at[k], t2r.at[s], step=slot_device(f)
        )
        copy.start()
        t2.append(copy)
    partner = s + 1 - 2 * (s % 2)
    to_partner = remote(
        sbuf.at[slot], spec.at[:, pl.ds(x0, B), pl.ds(y0, B)], t2s.at[0], t2r.at[s], step=partner
    )

    @pl.when(jnp.logical_not(active))
    def _():
        to_partner.start()

    @pl.when(active)
    def _():
        for c in range(2):
            spec[c, pl.ds(x0, B), pl.ds(y0, B), :] = sbuf[slot, c]
        for k in range(1, STEPS):
            d = (s + k) % STEPS
            dx, dy = origin(d)
            remote(
                sbuf.at[slot], spec.at[:, pl.ds(dx, B), pl.ds(dy, B)], t2s.at[0], t2r.at[d], step=d
            ).wait_recv()

    lane = lax.broadcasted_iota(jnp.int32, (8, NZ), 1)

    def z_sum(v):
        n = v.shape[0]
        at = jnp.concatenate([lane] * (n // 8), 0) if n > 8 else lane
        below = jnp.where(at == 0, 0.0, pltpu.roll(v, 1, 1))
        above = jnp.where(at == NZ - 1, 0.0, pltpu.roll(v, NZ - 1, 1))
        return below + above

    def neighbours(load, x, y, n):
        total = load(x - 1, y, n) + load(x + 1, y, n)
        total = total + (load(x, y - 1, n) + load(x, y + 1, n))
        return total + z_sum(load(x, y, n))

    p_end = 2.0 / (16 * GAMMA**15)
    ends_re = table([0.5 * p_end] + [p_end * v for v in cos_of[1:]], slot)
    ends_im = table([-0.5 * p_end] + [p_end * v for v in sin_of[1:]], slot)

    @pl.when(active)
    def _():
        def start(x, c):
            k1, k2, kb = kc[0, x], kc[1, x], kc[2, x]
            s0, s1 = spec[0, x], spec[1, x]
            uu[0, 0, x + 1, pl.ds(8, NY), :] = k1 * s0 - kb * s1
            uu[0, 1, x + 1, pl.ds(8, NY), :] = k2 * s1 + kb * s0
            return c

        lax.fori_loop(0, NX, start, 0, unroll=4)

        def sweep(k, c):
            old = k % 2
            for x in range(NX):
                nb = [
                    neighbours(
                        lambda px, py, n, q=q: uu[old, q, px, pl.ds(py, n), :], x + 1, 8, NY
                    )
                    for q in range(2)
                ]
                k1, k2, kb = kc[0, x], kc[1, x], kc[2, x]
                s0, s1 = spec[0, x] + nb[0], spec[1, x] + nb[1]
                uu[1 - old, 0, x + 1, pl.ds(8, NY), :] = k1 * s0 - kb * s1
                uu[1 - old, 1, x + 1, pl.ds(8, NY), :] = k2 * s1 + kb * s0
            return c

        lax.fori_loop(0, SWEEPS - 1, sweep, 0)

        def end(x, c):
            rows = pl.ds(8, NY)
            ee[x] = ends_re * uu[1, 0, x + 1, rows, :] + ends_im * uu[1, 1, x + 1, rows, :]
            return c

        lax.fori_loop(0, NX, end, 0, unroll=4)

        for k in range(1, STEPS):
            d = (s + k) % STEPS
            dx, dy = origin(d)
            remote(ee.at[pl.ds(dx, B), pl.ds(dy, B)], epart.at[slot], rss.at[k], rsr.at[slot], step=d).start()
        epart[slot] = ee[pl.ds(x0, B), pl.ds(y0, B), :]

    def slots_wait(wait):
        for k in range(1, SLOTS):
            f = (slot + k) % SLOTS
            wait(f, slot_device(f))
        pl.when(jnp.logical_not(active))(lambda: wait(slot, partner))

    block = (pl.ds(0, B), pl.ds(0, B))
    slots_wait(lambda f, d: remote(ee.at[block], epart.at[f], rss.at[0], rsr.at[f], step=d).wait_recv())
    for x in range(B):
        total = epart[0, x]
        for f in range(1, SLOTS):
            total = total + epart[f, x]
        ends[x] = total

    to_next = remote(ends, before, wns.at[0], wnr.at[0], win=(w + 1) % WINDOWS)
    to_next.start()
    to_next.wait_recv()
    later_window = jnp.where(w == 0, jnp.float32(0.0), jnp.float32(1.0 / COUPLING))
    for x in range(B):
        dext[B + x, pl.ds(B, B), :] = later_window * before[x] - (ALPHA / COUPLING) * ends[x]

    shifts = [(i, j) for i in (-1, 0, 1) for j in (-1, 0, 1) if (i, j) != (0, 0)]
    centre = dext.at[pl.ds(B, B), pl.ds(B, B)]
    halo = []
    for k, (i, j) in enumerate(shifts):
        d = ((bx + i + 4) % 4) * 4 + (by + j + 4) % 4
        copy = remote(
            centre, dext.at[pl.ds(B - B * i, B), pl.ds(B - B * j, B)], has.at[k], har.at[k], step=d
        )
        copy.start()
        halo.append(copy)

    @pl.when(active)
    def _():
        for k in range(1, STEPS):
            d = (s + k) % STEPS
            dx, dy = origin(d)
            remote(
                uu.at[1, :, pl.ds(dx + 1, B), pl.ds(pl.multiple_of(dy + 8, 8), B)],
                f1.at[slot], t3s.at[k], t3r.at[slot], step=d,
            ).start()
        for c in range(2):
            f1[slot, c] = uu[1, c, pl.ds(x0 + 1, B), pl.ds(pl.multiple_of(y0 + 8, 8), B), :]

    for copy in halo:
        copy.wait_recv()

    def wide_start(i, c):
        rows = pl.ds(0, 3 * B)
        d = dext[i, rows, :]
        for f in range(SLOTS):
            vv[0, f, 0, i, rows, :] = kx[f, 0, i, rows, :] * d
            vv[0, f, 1, i, rows, :] = kx[f, 1, i, rows, :] * d
        return c

    lax.fori_loop(0, 3 * B, wide_start, 0)
    for k in range(SWEEPS - 1):
        reach = SWEEPS - 2 - k
        old, new = k % 2, 1 - k % 2
        n = -(-(B + 2 * reach) // 8) * 8
        y = B - reach

        def wide(i, c, old=old, new=new, n=n, y=y):
            rows = pl.ds(y, n)
            d = dext[i, rows, :]
            for f in range(SLOTS):
                nb = [
                    neighbours(lambda px, py, m, q=q: vv[old, f, q, px, pl.ds(py, m), :], i, y, n)
                    for q in range(2)
                ]
                ka, kb = kx[f, 0, i, rows, :], kx[f, 1, i, rows, :]
                s0 = d + nb[0]
                if f == 0:
                    re, im = ka * s0, kb * (d + nb[1])
                else:
                    re, im = ka * s0 - kb * nb[1], ka * nb[1] + kb * s0
                vv[new, f, 0, i, rows, :] = re
                vv[new, f, 1, i, rows, :] = im
            return c

        lax.fori_loop(B - reach, 2 * B + reach, wide, 0, unroll=2)

    slots_wait(
        lambda f, d: remote(uu.at[1, :, pl.ds(0, B), pl.ds(0, B)], f1.at[f], t3s.at[0], t3r.at[f], step=d).wait_recv()
    )

    def untransform(x, c):
        total = [
            [f1[f, q, x] + vv[1, f, q, B + x, pl.ds(B, B), :] for q in range(2)] for f in range(SLOTS)
        ]
        spectrum = [(total[0][0], None)] + [tuple(v) for v in total[1:]] + [(total[0][1], None)]
        values = irdft(spectrum, STEPS)
        for t in range(STEPS):
            obuf[t, x] = values[t] * (GAMMA ** (-t) / STEPS)
        return c

    lax.fori_loop(0, B, untransform, 0)
    t4 = []
    for k in range(1, STEPS):
        d = (s + k) % STEPS
        copy = remote(obuf.at[d], out_ref.at[pl.ds(x0, B), pl.ds(y0, B)], t4s.at[k], t4r.at[s], step=d)
        copy.start()
        t4.append(copy)
    out_ref[pl.ds(x0, B), pl.ds(y0, B), :] = obuf[s]

    for copy in t1 + t2:
        copy.wait_send()
    pl.when(jnp.logical_not(active))(to_partner.wait_send)
    to_next.wait_send()
    for copy in halo:
        copy.wait_send()

    @pl.when(active)
    def _():
        for k in range(1, STEPS):
            d = (s + k) % STEPS
            remote(ee.at[block], epart.at[slot], rss.at[k], rsr.at[slot], step=d).wait_send()
            remote(
                uu.at[1, :, pl.ds(0, B), pl.ds(0, B)], f1.at[slot], t3s.at[k], t3r.at[slot], step=d
            ).wait_send()

    for k in range(1, STEPS):
        d = (s + k) % STEPS
        dx, dy = origin(d)
        remote(obuf.at[d], out_ref.at[pl.ds(dx, B), pl.ds(dy, B)], t4s.at[k], t4r.at[d], step=d).wait_recv()
    for copy in t4:
        copy.wait_send()


def per_device(initial_state, source, absorption):
    grid = (NX, NY, NZ)
    vmem = lambda *shape: pltpu.VMEM(shape, F32)
    dma = lambda n: pltpu.SemaphoreType.DMA((n,))
    result = pl.pallas_call(
        kernel,
        out_shape=jax.ShapeDtypeStruct(grid, F32),
        in_specs=[pl.BlockSpec(memory_space=pl.ANY)] * 3,
        out_specs=pl.BlockSpec(memory_space=pltpu.VMEM),
        scratch_shapes=[
            vmem(*grid),
            vmem(*grid),
            vmem(B, B, NZ),
            vmem(STEPS, B, B, NZ),
            vmem(SLOTS, 2, B, B, NZ),
            vmem(2, *grid),
            vmem(3, *grid),
            vmem(2, 2, NX + 2, NY + 16, NZ),
            vmem(*grid),
            vmem(SLOTS, B, B, NZ),
            vmem(B, B, NZ),
            vmem(B, B, NZ),
            vmem(3 * B, 4 * B, NZ),
            vmem(SLOTS, 2, 3 * B, 4 * B, NZ),
            vmem(2, SLOTS, 2, 3 * B, 4 * B, NZ),
            vmem(SLOTS, 2, B, B, NZ),
            vmem(STEPS, B, B, NZ),
            dma(3),
            dma(STEPS), dma(STEPS),
            dma(SLOTS), dma(STEPS),
            dma(STEPS), dma(SLOTS),
            dma(1), dma(1),
            dma(8), dma(8),
            dma(STEPS), dma(SLOTS),
            dma(STEPS), dma(STEPS),
        ],
        compiler_params=pltpu.CompilerParams(
            collective_id=0, has_side_effects=True, vmem_limit_bytes=60 * 2**20
        ),
        name="windows",
    )(source[0, 0], initial_state, absorption)
    return result[None, None]


def solution(mesh):
    return jax.shard_map(
        per_device,
        mesh=mesh,
        in_specs=(P(), P("win", "step", None, None, None), P()),
        out_specs=P("win", "step", None, None, None),
        check_vma=False,
    )
```

time: 212 us -> 70.2 us (0.33)
  the two profiles are of different devices: /device:TPU:32 before, /device:TPU:0 now
where the time goes in v1:
time: 70.2 us; the launch traced here: 68.9 us
  Pallas kernels  67 us (95%)
  local copies, waits for them, and re-layouts  1.87 us (3%)
    pallas_call x1, Pallas kernels, per_device(): pl.pallas_call(kernel, out_shape=jax.ShapeDtypeStruct(grid, F32), in_spec...  67 us
    unnamed x1, local copies, waits for them, and re-layouts  1.87 us

profile of v1, /device:TPU:0, one launch (start us, length us, event | category | flops | bytes accessed | tf_op | source)
XLA Modules:
  0.0 68.9 jit_solution(13224226508720995989)
XLA Ops:
  0.0 67.0 %windows.1 = f32[32,32,128]{2,1,0:T(8,128)} custom-call(f32[32,32,128]{2,1,0:T(8,128)} %bitcast.3, f32[32,32,128]{2,1,0:T(8,128)} %init_hbm.1, f32[32,32,128]{2,1,0:T(8,128)} %abs_hbm.1), custom_call_target="tpu_custom_call" | custom-call | tf_op jit(solution)/shard_map/windows/pallas_call | solution.py:477
  67.0 1.9 %copy.5 = f32[1,1,32,32,128]{4,3,2,1,0:T(8,128)} copy(f32[1,1,32,32,128]{4,3,2,1,0:T(8,128)} %bitcast.2) | data formatting | bytes 1048576

commit v2 on v1

--- a/solution.py
+++ b/solution.py
@@ -12,6 +12,9 @@
 STEPS = 16
 WINDOWS = 8
 SLOTS = 8
+PAIRS = 4
+GROUPS = (5, 6, 8, 7, 6, 10, 8)
+PITCH = 32
 ALPHA = 0.1
 COUPLING = 0.05
 GAMMA = ALPHA ** (1.0 / STEPS)
@@ -19,6 +22,8 @@
 B = 8
 MESH = pl.DeviceIdType.MESH
 F32 = jnp.float32
+BF16 = jnp.bfloat16
+HALF = NZ // 2
 
 
 def wpow(n, k):
@@ -111,6 +116,29 @@
     return times(c, s, re, im)
 
 
+def part(p, odd, q):
+    return p * 4 + odd * 2 + q
+
+
+def kz(odd):
+    return 16 + odd
+
+
+def dd(which):
+    return 18 + which
+
+
+def spread(v, pick, terms=3):
+    total = None
+    for k in range(terms):
+        part = v.astype(BF16)
+        product = jnp.dot(part, pick, preferred_element_type=F32)
+        total = product if total is None else total + product
+        if k < terms - 1:
+            v = v - part.astype(F32)
+    return total
+
+
 def table(values, index):
     out = jnp.float32(values[0])
     for k in range(1, len(values)):
@@ -120,7 +148,7 @@
 
 def kernel(
     src_hbm, init_hbm, abs_hbm, out_ref,
-    src, ab, init, tbuf, sbuf, spec, kc, uu, ee, epart, ends, before, dext, kx, vv, f1, obuf,
+    src, ab, init, tbuf, sbuf, spec, kc, uu, ee, epart, ends, before, dext, va, vb, kk, join, f1, obuf,
     lsem, t1s, t1r, t2s, t2r, rss, rsr, wns, wnr, has, har, t3s, t3r, t4s, t4r,
 ):
     s = lax.axis_index("step")
@@ -190,11 +218,12 @@
     def _():
         def plane(x, c):
             k1, k2, kb = coefficients(ab[x], c1, c2, sn)
-            kc[0, x], kc[1, x], kc[2, x] = k1, k2, kb
+            for n, value in enumerate((k1, k2, kb)):
+                kc[n, x, pl.ds(0, NY), :] = value
             return c
 
         lax.fori_loop(0, NX, plane, 0, unroll=4)
-        zero = jnp.zeros((48, NZ), F32)
+        zero = jnp.zeros((NY + 24, NZ), F32)
         zrow = jnp.zeros((8, NZ), F32)
         for p in range(2):
             for c in range(2):
@@ -209,30 +238,6 @@
             return c
 
         lax.fori_loop(1, NX + 1, rows, 0, unroll=4)
-
-    def wide_plane(i, c):
-        gx = x0 - B + i
-        inx = jnp.logical_and(gx >= 0, gx < NX)
-        gxc = jnp.clip(gx, 0, NX - 1)
-        for b in range(3):
-            gy = by - 1 + b
-            inside = jnp.logical_and(inx, jnp.logical_and(gy >= 0, gy < 4))
-            keep = jnp.where(inside, jnp.float32(1.0), jnp.float32(0.0))
-            a = ab[gxc, pl.ds(pl.multiple_of(jnp.clip(gy, 0, 3) * B, B), B), :]
-            for f in range(SLOTS):
-                if f == 0:
-                    first = keep * COUPLING / (a + (1.0 + 6.0 * COUPLING - GAMMA))
-                    second = keep * COUPLING / (a + (1.0 + 6.0 * COUPLING + GAMMA))
-                else:
-                    r = a + (1.0 + 6.0 * COUPLING - GAMMA * cos_of[f])
-                    im = GAMMA * sin_of[f]
-                    scale = keep * COUPLING / (r * r + im * im)
-                    first, second = r * scale, -im * scale
-                kx[f, 0, i, pl.ds(b * B, B), :] = first
-                kx[f, 1, i, pl.ds(b * B, B), :] = second
-        return c
-
-    lax.fori_loop(0, 3 * B, wide_plane, 0)
 
     for k in range(1, STEPS):
         d = (s - k) % STEPS
@@ -271,6 +276,57 @@
     def _():
         to_partner.start()
 
+
+    wide_lane = lax.broadcasted_iota(jnp.int32, (3 * B, NZ), 1)
+    low = wide_lane < HALF
+    pick_z = lax.broadcasted_iota(jnp.int32, (NZ, 2 * NZ), 0)
+    pick_l = lax.broadcasted_iota(jnp.int32, (NZ, 2 * NZ), 1)
+    pick = jnp.where(pick_z == 2 * (pick_l % HALF) + pick_l // NZ, 1.0, 0.0).astype(BF16)
+    join_r = lax.broadcasted_iota(jnp.int32, (2 * NZ, 2 * NZ), 0)
+    join_c = lax.broadcasted_iota(jnp.int32, (2 * NZ, 2 * NZ), 1)
+    goes = ((join_r // HALF) % 2) * NZ + 2 * (join_r % HALF) + join_r // NZ
+    join[...] = jnp.where(join_c == goes, 1.0, 0.0).astype(BF16)
+
+    def at(a, b):
+        return jnp.where(low, jnp.float32(a), jnp.float32(b))
+
+    def turned(v, odd):
+        lanes = wide_lane[: v.shape[0]] % HALF
+        if odd:
+            return jnp.where(lanes == 0, 0.0, pltpu.roll(v, 1, 1))
+        return jnp.where(lanes == HALF - 1, 0.0, pltpu.roll(v, NZ - 1, 1))
+
+    def wide_plane(i, c):
+        gx = x0 - B + i
+        inx = jnp.logical_and(gx >= 0, gx < NX)
+        gxc = jnp.clip(gx, 0, NX - 1)
+        tiles, keeps = [], []
+        for b in range(3):
+            gy = by - 1 + b
+            inside = jnp.logical_and(inx, jnp.logical_and(gy >= 0, gy < 4))
+            keep = jnp.where(inside, jnp.float32(COUPLING), jnp.float32(0.0))
+            tiles.append(ab[gxc, pl.ds(pl.multiple_of(jnp.clip(gy, 0, 3) * B, B), B), :])
+            keeps.append(jnp.full((B, NZ), keep, F32))
+        both = spread(jnp.concatenate(tiles, 0), pick)
+        keep = jnp.concatenate(keeps, 0)
+        rows = pl.ds(pl.multiple_of(i * PITCH, PITCH), 3 * B)
+        for odd in range(2):
+            base = both[:, odd * NZ : (odd + 1) * NZ] + (1.0 + 6.0 * COUPLING)
+            for p in range(PAIRS):
+                q = p + PAIRS
+                r = base - at(GAMMA * cos_of[p], GAMMA * cos_of[q])
+                im = at(GAMMA * sin_of[p], GAMMA * sin_of[q])
+                scale = keep / (r * r + im * im)
+                ka, kb = r * scale, -im * scale
+                if p == 0:
+                    r2 = base - at(-GAMMA, GAMMA * cos_of[q])
+                    k2 = r2 * (keep / (r2 * r2 + im * im))
+                    kk[kz(odd), rows, :] = k2
+                kk[part(p, odd, 0), rows, :], kk[part(p, odd, 1), rows, :] = ka, kb
+        return c
+
+    lax.fori_loop(1, 3 * B - 1, wide_plane, 0)
+
     @pl.when(active)
     def _():
         for c in range(2):
@@ -303,8 +359,8 @@
     @pl.when(active)
     def _():
         def start(x, c):
-            k1, k2, kb = kc[0, x], kc[1, x], kc[2, x]
-            s0, s1 = spec[0, x], spec[1, x]
+            k1, k2, kb = (kc[n, x, pl.ds(0, NY), :] for n in range(3))
+            s0, s1 = (spec[n, x, pl.ds(0, NY), :] for n in range(2))
             uu[0, 0, x + 1, pl.ds(8, NY), :] = k1 * s0 - kb * s1
             uu[0, 1, x + 1, pl.ds(8, NY), :] = k2 * s1 + kb * s0
             return c
@@ -320,8 +376,8 @@
                     )
                     for q in range(2)
                 ]
-                k1, k2, kb = kc[0, x], kc[1, x], kc[2, x]
-                s0, s1 = spec[0, x] + nb[0], spec[1, x] + nb[1]
+                k1, k2, kb = (kc[n, x, pl.ds(0, NY), :] for n in range(3))
+                s0, s1 = (spec[n, x, pl.ds(0, NY), :] + nb[n] for n in range(2))
                 uu[1 - old, 0, x + 1, pl.ds(8, NY), :] = k1 * s0 - kb * s1
                 uu[1 - old, 1, x + 1, pl.ds(8, NY), :] = k2 * s1 + kb * s0
             return c
@@ -357,22 +413,6 @@
 
     to_next = remote(ends, before, wns.at[0], wnr.at[0], win=(w + 1) % WINDOWS)
     to_next.start()
-    to_next.wait_recv()
-    later_window = jnp.where(w == 0, jnp.float32(0.0), jnp.float32(1.0 / COUPLING))
-    for x in range(B):
-        dext[B + x, pl.ds(B, B), :] = later_window * before[x] - (ALPHA / COUPLING) * ends[x]
-
-    shifts = [(i, j) for i in (-1, 0, 1) for j in (-1, 0, 1) if (i, j) != (0, 0)]
-    centre = dext.at[pl.ds(B, B), pl.ds(B, B)]
-    halo = []
-    for k, (i, j) in enumerate(shifts):
-        d = ((bx + i + 4) % 4) * 4 + (by + j + 4) % 4
-        copy = remote(
-            centre, dext.at[pl.ds(B - B * i, B), pl.ds(B - B * j, B)], has.at[k], har.at[k], step=d
-        )
-        copy.start()
-        halo.append(copy)
-
     @pl.when(active)
     def _():
         for k in range(1, STEPS):
@@ -385,56 +425,105 @@
         for c in range(2):
             f1[slot, c] = uu[1, c, pl.ds(x0 + 1, B), pl.ds(pl.multiple_of(y0 + 8, 8), B), :]
 
+    to_next.wait_recv()
+    later_window = jnp.where(w == 0, jnp.float32(0.0), jnp.float32(1.0 / COUPLING))
+    change = later_window * before[...] - (ALPHA / COUPLING) * ends[...]
+    pack = jnp.where(
+        pick_z[:, :NZ] == 2 * (pick_l[:, :NZ] % HALF) + pick_l[:, :NZ] // HALF, 1.0, 0.0
+    ).astype(BF16)
+    dext[pl.ds(B, B), pl.ds(B, B), :] = spread(change.reshape(B * B, NZ), pack).reshape(B, B, NZ)
+
+    shifts = [(i, j) for i in (-1, 0, 1) for j in (-1, 0, 1) if (i, j) != (0, 0)]
+    centre = dext.at[pl.ds(B, B), pl.ds(B, B)]
+    halo = []
+    for k, (i, j) in enumerate(shifts):
+        d = ((bx + i + 4) % 4) * 4 + (by + j + 4) % 4
+        copy = remote(
+            centre, dext.at[pl.ds(B - B * i, B), pl.ds(B - B * j, B)], has.at[k], har.at[k], step=d
+        )
+        copy.start()
+        halo.append(copy)
+
     for copy in halo:
         copy.wait_recv()
 
     def wide_start(i, c):
-        rows = pl.ds(0, 3 * B)
-        d = dext[i, rows, :]
-        for f in range(SLOTS):
-            vv[0, f, 0, i, rows, :] = kx[f, 0, i, rows, :] * d
-            vv[0, f, 1, i, rows, :] = kx[f, 1, i, rows, :] * d
+        rows = pl.ds(pl.multiple_of(i * PITCH, PITCH), 3 * B)
+        v = dext[i, pl.ds(0, 3 * B), :]
+        swapped = pltpu.roll(v, HALF, 1)
+        d = [jnp.where(low, v, swapped), jnp.where(low, swapped, v)]
+        for odd in range(2):
+            kk[dd(odd), rows, :] = d[odd]
+            kk[dd(2 + odd), rows, :] = jnp.where(low, d[odd], 0.0)
+            for p in range(PAIRS):
+                second = kk[part(p, odd, 1), rows, :]
+                if p == 0:
+                    second = jnp.where(low, kk[kz(odd), rows, :], second)
+                va[part(p, odd, 0), rows, :] = kk[part(p, odd, 0), rows, :] * d[odd]
+                va[part(p, odd, 1), rows, :] = second * d[odd]
         return c
 
-    lax.fori_loop(0, 3 * B, wide_start, 0)
+    lax.fori_loop(1, 3 * B - 1, wide_start, 0)
+    zero_row = s // STEPS
     for k in range(SWEEPS - 1):
         reach = SWEEPS - 2 - k
-        old, new = k % 2, 1 - k % 2
+        vo, vn = (va, vb) if k % 2 == 0 else (vb, va)
         n = -(-(B + 2 * reach) // 8) * 8
-        y = B - reach
-
-        def wide(i, c, old=old, new=new, n=n, y=y):
-            rows = pl.ds(y, n)
-            d = dext[i, rows, :]
-            for f in range(SLOTS):
-                nb = [
-                    neighbours(lambda px, py, m, q=q: vv[old, f, q, px, pl.ds(py, m), :], i, y, n)
-                    for q in range(2)
-                ]
-                ka, kb = kx[f, 0, i, rows, :], kx[f, 1, i, rows, :]
-                s0 = d + nb[0]
-                if f == 0:
-                    re, im = ka * s0, kb * (d + nb[1])
-                else:
-                    re, im = ka * s0 - kb * nb[1], ka * nb[1] + kb * s0
-                vv[new, f, 0, i, rows, :] = re
-                vv[new, f, 1, i, rows, :] = im
+        first_row = zero_row + (B - reach)
+        group = GROUPS[k]
+
+        def compute(start, n=n, vo=vo, vn=vn):
+            rows = pl.ds(start, n)
+            around = [pl.ds(start + shift, n) for shift in (-PITCH, PITCH, -1, 1)]
+            for p in range(PAIRS):
+                middle = [[vo[part(p, odd, q), rows, :] for q in range(2)] for odd in range(2)]
+                for odd in range(2):
+                    nb = []
+                    for q in range(2):
+                        here, other = part(p, odd, q), middle[1 - odd][q]
+                        t = vo[here, around[0], :] + vo[here, around[1], :]
+                        t = t + (vo[here, around[2], :] + vo[here, around[3], :])
+                        nb.append((t + other) + turned(other, 1 - odd))
+                    ka, kb = kk[part(p, odd, 0), rows, :], kk[part(p, odd, 1), rows, :]
+                    s0, s1, k2 = kk[dd(odd), rows, :] + nb[0], nb[1], ka
+                    if p == 0:
+                        s1, k2 = s1 + kk[dd(2 + odd), rows, :], kk[kz(odd), rows, :]
+                    vn[part(p, odd, 0), rows, :] = ka * s0 - kb * s1
+                    vn[part(p, odd, 1), rows, :] = k2 * s1 + kb * s0
+
+        def wide(j, c, reach=reach, compute=compute, group=group, first_row=first_row):
+            start = (B - reach + group * j) * PITCH + first_row
+            for m in range(group):
+                for tile in range(n // 8):
+                    compute(start + m * PITCH + tile * 8, 8)
             return c
 
-        lax.fori_loop(B - reach, 2 * B + reach, wide, 0, unroll=2)
+        lax.fori_loop(0, (B + 2 * reach) // group, wide, 0)
 
     slots_wait(
         lambda f, d: remote(uu.at[1, :, pl.ds(0, B), pl.ds(0, B)], f1.at[f], t3s.at[0], t3r.at[f], step=d).wait_recv()
     )
 
+    for p in range(PAIRS):
+        for q in range(2):
+            mixed = jnp.concatenate(
+                [
+                    jnp.concatenate([vb[part(p, odd, q), pl.ds((B + x) * PITCH + B, B), :] for x in range(B)], 0)
+                    for odd in range(2)
+                ],
+                1,
+            )
+            natural = spread(mixed, join[...], 2)
+            for h in range(2):
+                f = p + h * PAIRS
+                f1[f, q] = f1[f, q] + natural[:, h * NZ : (h + 1) * NZ].reshape(B, B, NZ)
+
     def untransform(x, c):
-        total = [
-            [f1[f, q, x] + vv[1, f, q, B + x, pl.ds(B, B), :] for q in range(2)] for f in range(SLOTS)
-        ]
+        total = [[f1[f, q, x] for q in range(2)] for f in range(SLOTS)]
         spectrum = [(total[0][0], None)] + [tuple(v) for v in total[1:]] + [(total[0][1], None)]
         values = irdft(spectrum, STEPS)
         for t in range(STEPS):
-            obuf[t, x] = values[t] * (GAMMA ** (-t) / STEPS)
+            obuf[t, x] = values[t]
         return c
 
     lax.fori_loop(0, B, untransform, 0)
@@ -476,7 +565,7 @@
     dma = lambda n: pltpu.SemaphoreType.DMA((n,))
     result = pl.pallas_call(
         kernel,
-        out_shape=jax.ShapeDtypeStruct(grid, F32),
+        out_shape=pltpu.VMEM(grid, F32),
         in_specs=[pl.BlockSpec(memory_space=pl.ANY)] * 3,
         out_specs=pl.BlockSpec(memory_space=pltpu.VMEM),
         scratch_shapes=[
@@ -485,16 +574,18 @@
             vmem(B, B, NZ),
             vmem(STEPS, B, B, NZ),
             vmem(SLOTS, 2, B, B, NZ),
-            vmem(2, *grid),
-            vmem(3, *grid),
-            vmem(2, 2, NX + 2, NY + 16, NZ),
+            vmem(2, NX, NY + 8, NZ),
+            vmem(4, NX, NY + 8, NZ),
+            vmem(2, 2, NX + 4, NY + 24, NZ),
             vmem(*grid),
             vmem(SLOTS, B, B, NZ),
             vmem(B, B, NZ),
             vmem(B, B, NZ),
             vmem(3 * B, 4 * B, NZ),
-            vmem(SLOTS, 2, 3 * B, 4 * B, NZ),
-            vmem(2, SLOTS, 2, 3 * B, 4 * B, NZ),
+            vmem(16, 3 * B * PITCH + 8, NZ),
+            vmem(16, 3 * B * PITCH + 8, NZ),
+            vmem(24, 3 * B * PITCH + 8, NZ),
+            pltpu.VMEM((2 * NZ, 2 * NZ), BF16),
             vmem(SLOTS, 2, B, B, NZ),
             vmem(STEPS, B, B, NZ),
             dma(3),
@@ -511,7 +602,8 @@
         ),
         name="windows",
     )(source[0, 0], initial_state, absorption)
-    return result[None, None]
+    moment = lax.axis_index("step").astype(F32)
+    return (result * (GAMMA ** (-moment) / STEPS))[None, None]
 
 
 def solution(mesh):

time: 70.2 us -> 64.1 us (0.913)
  Pallas kernels: 67 us -> 62.3 us
  local copies, waits for them, and re-layouts: 1.87 us -> 0 us
  other arithmetic: 0 us -> 0.84 us
    pallas_call x1, Pallas kernels: 67 us -> 62.3 us  [per_device(): pl.pallas_call(kernel, out_shape=pltpu.VMEM(grid, F32), in_specs=[pl.Bloc...]
    unnamed x1 -> x0, local copies, waits for them, and re-layouts: 1.87 us -> none
    broadcast_in_dim x0 -> x1, other arithmetic: none -> 0.84 us  [per_device(): return (result * (GAMMA ** (-moment) / STEPS))[None, None]]
where the time goes in v2:
time: 64.1 us; the launch traced here: 63.2 us
  Pallas kernels  62.3 us (97%)
  other arithmetic  0.84 us (1%)
    pallas_call x1, Pallas kernels, per_device(): pl.pallas_call(kernel, out_shape=pltpu.VMEM(grid, F32), in_specs=[pl.Bloc...  62.3 us

profile of v2, /device:TPU:0, one launch (start us, length us, event | category | flops | bytes accessed | tf_op | source)
XLA Modules:
  0.0 63.2 jit_solution(16266452945894534559)
XLA Ops:
  0.0 62.3 %windows.1 = f32[32,32,128]{2,1,0:T(8,128)S(1)} custom-call(f32[32,32,128]{2,1,0:T(8,128)} %bitcast.3, f32[32,32,128]{2,1,0:T(8,128)} %init_hbm.1, f32[32,32,128]{2,1,0:T(8,128)} %abs_hbm.1), custom_call_target="tpu_custom_call" | custom-call | tf_op jit(solution)/shard_map/windows/pallas_call | solution.py:566
  62.3 0.8 %multiply_bitcast_fusion = f32[1,1,32,32,128]{4,3,2,1,0:T(8,128)} fusion(f32[32,32,128]{2,1,0:T(8,128)S(1)} %windows.1, f32[]{:T(128)S(6)} %div.3), kind=kLoop, calls=%fused_computation | loop fusion | flops 131072 | bytes 1048580 | tf_op jit(solution)/shard_map/broadcast_in_dim | solution.py:606

commit v3 on v2

--- a/solution.py
+++ b/solution.py
@@ -13,7 +13,6 @@
 WINDOWS = 8
 SLOTS = 8
 PAIRS = 4
-GROUPS = (5, 6, 8, 7, 6, 10, 8)
 PITCH = 32
 ALPHA = 0.1
 COUPLING = 0.05
@@ -24,6 +23,18 @@
 F32 = jnp.float32
 BF16 = jnp.bfloat16
 HALF = NZ // 2
+
+
+def hops(d):
+    return min(d[0], 4 - d[0]) + min(d[1], 4 - d[1])
+
+
+OFFSETS = [(i, j) for i in (2, 1, 3, 0) for j in (2, 1, 3, 0) if (i, j) != (0, 0)]
+OFFSETS.sort(key=lambda d: -hops(d))
+EVEN = [d for d in OFFSETS if sum(d) % 2 == 0]
+ODD = [d for d in OFFSETS if sum(d) % 2 == 1]
+PARTS = 2
+PB = B // PARTS
 
 
 def wpow(n, k):
@@ -124,8 +135,12 @@
     return 16 + odd
 
 
-def dd(which):
-    return 18 + which
+def dz(odd):
+    return 18 + odd
+
+
+def dd(odd):
+    return 24 + odd
 
 
 def spread(v, pick, terms=3):
@@ -173,6 +188,9 @@
             device_id_type=MESH,
         )
 
+    def device(shift):
+        return (bx + shift[0]) % 4 * 4 + (by + shift[1]) % 4
+
     load_src = pltpu.make_async_copy(src_hbm, src, lsem.at[0])
     load_abs = pltpu.make_async_copy(abs_hbm, ab, lsem.at[1])
     load_init = pltpu.make_async_copy(init_hbm.at[pl.ds(x0, B), pl.ds(y0, B)], init, lsem.at[2])
@@ -189,12 +207,16 @@
     load_src.wait()
 
     t1 = []
-    for k in range(1, STEPS):
-        d = (s + k) % STEPS
-        dx, dy = origin(d)
-        copy = remote(src.at[pl.ds(dx, B), pl.ds(dy, B)], tbuf.at[s], t1s.at[k], t1r.at[s], step=d)
-        copy.start()
-        t1.append(copy)
+    for h in range(PARTS):
+        for k, shift in enumerate(OFFSETS):
+            d = device(shift)
+            dx, dy = origin(d)
+            copy = remote(
+                src.at[pl.ds(dx + h * PB, PB), pl.ds(dy, B)], tbuf.at[s, pl.ds(h * PB, PB)],
+                t1s.at[k, h], t1r.at[s, h], step=d,
+            )
+            copy.start()
+            t1.append(copy)
     load_init.wait()
     load_abs.wait()
     tbuf[s] = src[pl.ds(x0, B), pl.ds(y0, B), :]
@@ -239,9 +261,6 @@
 
         lax.fori_loop(1, NX + 1, rows, 0, unroll=4)
 
-    for k in range(1, STEPS):
-        d = (s - k) % STEPS
-        remote(src.at[pl.ds(0, B), pl.ds(0, B)], tbuf.at[d], t1s.at[k], t1r.at[d], step=d).wait_recv()
     first_window = jnp.where(w == 0, jnp.float32(1.0), jnp.float32(0.0))
 
     def transform(x, c):
@@ -257,25 +276,36 @@
             sbuf[f, 0, x], sbuf[f, 1, x] = out[f]
         return c
 
-    lax.fori_loop(0, B, transform, 0)
-
-    t2 = []
-    for k in range(1, SLOTS):
-        f = (slot + k) % SLOTS
-        copy = remote(
-            sbuf.at[f], spec.at[:, pl.ds(x0, B), pl.ds(y0, B)], t2s.at[k], t2r.at[s], step=slot_device(f)
+    def to_slot(k, h, shift):
+        d = device(shift)
+        half = pl.ds(x0 + h * PB, PB)
+        return remote(
+            sbuf.at[d // 2, :, pl.ds(h * PB, PB)], spec.at[:, half, pl.ds(y0, B)],
+            t2s.at[k, h], t2r.at[s, h], step=d,
         )
-        copy.start()
-        t2.append(copy)
-    partner = s + 1 - 2 * (s % 2)
-    to_partner = remote(
-        sbuf.at[slot], spec.at[:, pl.ds(x0, B), pl.ds(y0, B)], t2s.at[0], t2r.at[s], step=partner
-    )
-
-    @pl.when(jnp.logical_not(active))
-    def _():
-        to_partner.start()
-
+
+    def send_to_slots(act):
+        def run(h):
+            @pl.when(active)
+            def _():
+                for k, shift in enumerate(EVEN):
+                    act(to_slot(k, h, shift))
+
+            @pl.when(jnp.logical_not(active))
+            def _():
+                for k, shift in enumerate(ODD):
+                    act(to_slot(k, h, shift))
+
+        return run
+
+    for h in range(PARTS):
+        for k in range(1, STEPS):
+            d = (s - k) % STEPS
+            remote(
+                src.at[pl.ds(0, PB), pl.ds(0, B)], tbuf.at[d, pl.ds(h * PB, PB)], t1s.at[0, h], t1r.at[d, h], step=d
+            ).wait_recv()
+        lax.fori_loop(h * PB, (h + 1) * PB, transform, 0)
+        send_to_slots(lambda copy: copy.start())(h)
 
     wide_lane = lax.broadcasted_iota(jnp.int32, (3 * B, NZ), 1)
     low = wide_lane < HALF
@@ -323,6 +353,8 @@
                     k2 = r2 * (keep / (r2 * r2 + im * im))
                     kk[kz(odd), rows, :] = k2
                 kk[part(p, odd, 0), rows, :], kk[part(p, odd, 1), rows, :] = ka, kb
+                if p == 2:
+                    kk[4 + kz(odd), rows, :], kk[4 + dz(odd), rows, :] = ka, jnp.zeros_like(ka)
         return c
 
     lax.fori_loop(1, 3 * B - 1, wide_plane, 0)
@@ -331,12 +363,14 @@
     def _():
         for c in range(2):
             spec[c, pl.ds(x0, B), pl.ds(y0, B), :] = sbuf[slot, c]
-        for k in range(1, STEPS):
-            d = (s + k) % STEPS
+        for shift in reversed(OFFSETS):
+            d = device(shift)
             dx, dy = origin(d)
-            remote(
-                sbuf.at[slot], spec.at[:, pl.ds(dx, B), pl.ds(dy, B)], t2s.at[0], t2r.at[d], step=d
-            ).wait_recv()
+            for h in range(PARTS):
+                remote(
+                    sbuf.at[slot, :, pl.ds(0, PB)], spec.at[:, pl.ds(dx + h * PB, PB), pl.ds(dy, B)],
+                    t2s.at[0, h], t2r.at[d, h], step=d,
+                ).wait_recv()
 
     lane = lax.broadcasted_iota(jnp.int32, (8, NZ), 1)
 
@@ -391,11 +425,13 @@
 
         lax.fori_loop(0, NX, end, 0, unroll=4)
 
-        for k in range(1, STEPS):
-            d = (s + k) % STEPS
+        for k, shift in enumerate(OFFSETS):
+            d = device(shift)
             dx, dy = origin(d)
             remote(ee.at[pl.ds(dx, B), pl.ds(dy, B)], epart.at[slot], rss.at[k], rsr.at[slot], step=d).start()
         epart[slot] = ee[pl.ds(x0, B), pl.ds(y0, B), :]
+
+    partner = s + 1 - 2 * (s % 2)
 
     def slots_wait(wait):
         for k in range(1, SLOTS):
@@ -413,18 +449,6 @@
 
     to_next = remote(ends, before, wns.at[0], wnr.at[0], win=(w + 1) % WINDOWS)
     to_next.start()
-    @pl.when(active)
-    def _():
-        for k in range(1, STEPS):
-            d = (s + k) % STEPS
-            dx, dy = origin(d)
-            remote(
-                uu.at[1, :, pl.ds(dx + 1, B), pl.ds(pl.multiple_of(dy + 8, 8), B)],
-                f1.at[slot], t3s.at[k], t3r.at[slot], step=d,
-            ).start()
-        for c in range(2):
-            f1[slot, c] = uu[1, c, pl.ds(x0 + 1, B), pl.ds(pl.multiple_of(y0 + 8, 8), B), :]
-
     to_next.wait_recv()
     later_window = jnp.where(w == 0, jnp.float32(0.0), jnp.float32(1.0 / COUPLING))
     change = later_window * before[...] - (ALPHA / COUPLING) * ends[...]
@@ -447,6 +471,19 @@
     for copy in halo:
         copy.wait_recv()
 
+    @pl.when(active)
+    def _():
+        for k, shift in enumerate(OFFSETS):
+            d = device(shift)
+            dx, dy = origin(d)
+            remote(
+                uu.at[1, :, pl.ds(dx + 1, B), pl.ds(pl.multiple_of(dy + 8, 8), B)],
+                f1.at[slot], t3s.at[k], t3r.at[slot], step=d,
+            ).start()
+        for c in range(2):
+            f1[slot, c] = uu[1, c, pl.ds(x0 + 1, B), pl.ds(pl.multiple_of(y0 + 8, 8), B), :]
+
+
     def wide_start(i, c):
         rows = pl.ds(pl.multiple_of(i * PITCH, PITCH), 3 * B)
         v = dext[i, pl.ds(0, 3 * B), :]
@@ -454,7 +491,7 @@
         d = [jnp.where(low, v, swapped), jnp.where(low, swapped, v)]
         for odd in range(2):
             kk[dd(odd), rows, :] = d[odd]
-            kk[dd(2 + odd), rows, :] = jnp.where(low, d[odd], 0.0)
+            kk[dz(odd), rows, :] = jnp.where(low, d[odd], 0.0)
             for p in range(PAIRS):
                 second = kk[part(p, odd, 1), rows, :]
                 if p == 0:
@@ -468,37 +505,35 @@
     for k in range(SWEEPS - 1):
         reach = SWEEPS - 2 - k
         vo, vn = (va, vb) if k % 2 == 0 else (vb, va)
-        n = -(-(B + 2 * reach) // 8) * 8
-        first_row = zero_row + (B - reach)
-        group = GROUPS[k]
-
-        def compute(start, n=n, vo=vo, vn=vn):
-            rows = pl.ds(start, n)
-            around = [pl.ds(start + shift, n) for shift in (-PITCH, PITCH, -1, 1)]
-            for p in range(PAIRS):
-                middle = [[vo[part(p, odd, q), rows, :] for q in range(2)] for odd in range(2)]
-                for odd in range(2):
-                    nb = []
-                    for q in range(2):
-                        here, other = part(p, odd, q), middle[1 - odd][q]
-                        t = vo[here, around[0], :] + vo[here, around[1], :]
-                        t = t + (vo[here, around[2], :] + vo[here, around[3], :])
-                        nb.append((t + other) + turned(other, 1 - odd))
-                    ka, kb = kk[part(p, odd, 0), rows, :], kk[part(p, odd, 1), rows, :]
-                    s0, s1, k2 = kk[dd(odd), rows, :] + nb[0], nb[1], ka
-                    if p == 0:
-                        s1, k2 = s1 + kk[dd(2 + odd), rows, :], kk[kz(odd), rows, :]
-                    vn[part(p, odd, 0), rows, :] = ka * s0 - kb * s1
-                    vn[part(p, odd, 1), rows, :] = k2 * s1 + kb * s0
-
-        def wide(j, c, reach=reach, compute=compute, group=group, first_row=first_row):
-            start = (B - reach + group * j) * PITCH + first_row
-            for m in range(group):
-                for tile in range(n // 8):
-                    compute(start + m * PITCH + tile * 8, 8)
+        places = []
+        for i in range(B - reach, 2 * B + reach):
+            rest = reach - max(B - i, i - 2 * B + 1, 0)
+            places += [i * PITCH + B - rest + 8 * tile for tile in range(-(-(B + 2 * rest) // 8))]
+
+        def wide(g, c, vo=vo, vn=vn, places=places):
+            for place in places:
+                start = place + zero_row
+                rows = pl.ds(start, 8)
+                around = [pl.ds(start + shift, 8) for shift in (-PITCH, PITCH, -1, 1)]
+                for p in range(2):
+                    first = 8 * g
+                    middle = [[vo[first + part(p, odd, q), rows, :] for q in range(2)] for odd in range(2)]
+                    for odd in range(2):
+                        nb = []
+                        for q in range(2):
+                            here, other = first + part(p, odd, q), middle[1 - odd][q]
+                            t = vo[here, around[0], :] + vo[here, around[1], :]
+                            t = t + (vo[here, around[2], :] + vo[here, around[3], :])
+                            nb.append((t + other) + turned(other, 1 - odd))
+                        ka, kb = kk[first + part(p, odd, 0), rows, :], kk[first + part(p, odd, 1), rows, :]
+                        s0, s1, k2 = kk[dd(odd), rows, :] + nb[0], nb[1], ka
+                        if p == 0:
+                            s1, k2 = s1 + kk[4 * g + dz(odd), rows, :], kk[4 * g + kz(odd), rows, :]
+                        vn[first + part(p, odd, 0), rows, :] = ka * s0 - kb * s1
+                        vn[first + part(p, odd, 1), rows, :] = k2 * s1 + kb * s0
             return c
 
-        lax.fori_loop(0, (B + 2 * reach) // group, wide, 0)
+        lax.fori_loop(0, 2, wide, 0)
 
     slots_wait(
         lambda f, d: remote(uu.at[1, :, pl.ds(0, B), pl.ds(0, B)], f1.at[f], t3s.at[0], t3r.at[f], step=d).wait_recv()
@@ -528,24 +563,25 @@
 
     lax.fori_loop(0, B, untransform, 0)
     t4 = []
-    for k in range(1, STEPS):
-        d = (s + k) % STEPS
+    for k, shift in enumerate(OFFSETS):
+        d = device(shift)
         copy = remote(obuf.at[d], out_ref.at[pl.ds(x0, B), pl.ds(y0, B)], t4s.at[k], t4r.at[s], step=d)
         copy.start()
         t4.append(copy)
     out_ref[pl.ds(x0, B), pl.ds(y0, B), :] = obuf[s]
 
-    for copy in t1 + t2:
+    for copy in t1:
         copy.wait_send()
-    pl.when(jnp.logical_not(active))(to_partner.wait_send)
+    for h in range(PARTS):
+        send_to_slots(lambda copy: copy.wait_send())(h)
     to_next.wait_send()
     for copy in halo:
         copy.wait_send()
 
     @pl.when(active)
     def _():
-        for k in range(1, STEPS):
-            d = (s + k) % STEPS
+        for k, shift in enumerate(OFFSETS):
+            d = device(shift)
             remote(ee.at[block], epart.at[slot], rss.at[k], rsr.at[slot], step=d).wait_send()
             remote(
                 uu.at[1, :, pl.ds(0, B), pl.ds(0, B)], f1.at[slot], t3s.at[k], t3r.at[slot], step=d
@@ -562,7 +598,7 @@
 def per_device(initial_state, source, absorption):
     grid = (NX, NY, NZ)
     vmem = lambda *shape: pltpu.VMEM(shape, F32)
-    dma = lambda n: pltpu.SemaphoreType.DMA((n,))
+    dma = lambda *n: pltpu.SemaphoreType.DMA(n)
     result = pl.pallas_call(
         kernel,
         out_shape=pltpu.VMEM(grid, F32),
@@ -584,13 +620,13 @@
             vmem(3 * B, 4 * B, NZ),
             vmem(16, 3 * B * PITCH + 8, NZ),
             vmem(16, 3 * B * PITCH + 8, NZ),
-            vmem(24, 3 * B * PITCH + 8, NZ),
+            vmem(28, 3 * B * PITCH + 8, NZ),
             pltpu.VMEM((2 * NZ, 2 * NZ), BF16),
             vmem(SLOTS, 2, B, B, NZ),
             vmem(STEPS, B, B, NZ),
             dma(3),
-            dma(STEPS), dma(STEPS),
-            dma(SLOTS), dma(STEPS),
+            dma(STEPS, PARTS), dma(STEPS, PARTS),
+            dma(SLOTS, PARTS), dma(STEPS, PARTS),
             dma(STEPS), dma(SLOTS),
             dma(1), dma(1),
             dma(8), dma(8),

time: 64.1 us -> 57.7 us (0.900); the launches traced: 63.2 us -> 57.5 us
  Pallas kernels: 62.3 us -> 56.6 us
    pallas_call x1, Pallas kernels: 62.3 us -> 56.6 us  [per_device(): pl.pallas_call(kernel, out_shape=pltpu.VMEM(grid, F32), in_specs=[pl.Bloc...]
where the time goes in v3:
time: 57.7 us; the launch traced here: 57.5 us
  Pallas kernels  56.6 us (98%)
  other arithmetic  0.84 us (1%)
    pallas_call x1, Pallas kernels, per_device(): pl.pallas_call(kernel, out_shape=pltpu.VMEM(grid, F32), in_specs=[pl.Bloc...  56.6 us

profile of v3, /device:TPU:0, one launch (start us, length us, event | category | flops | bytes accessed | tf_op | source)
XLA Modules:
  0.0 57.5 jit_solution(13111510427558984498)
XLA Ops:
  0.0 56.6 %windows.1 = f32[32,32,128]{2,1,0:T(8,128)S(1)} custom-call(f32[32,32,128]{2,1,0:T(8,128)} %bitcast.3, f32[32,32,128]{2,1,0:T(8,128)} %init_hbm.1, f32[32,32,128]{2,1,0:T(8,128)} %abs_hbm.1), custom_call_target="tpu_custom_call" | custom-call | tf_op jit(solution)/shard_map/windows/pallas_call | solution.py:602
  56.7 0.8 %multiply_bitcast_fusion = f32[1,1,32,32,128]{4,3,2,1,0:T(8,128)} fusion(f32[32,32,128]{2,1,0:T(8,128)S(1)} %windows.1, f32[]{:T(128)S(6)} %div.3), kind=kLoop, calls=%fused_computation | loop fusion | flops 131072 | bytes 1048580 | tf_op jit(solution)/shard_map/broadcast_in_dim | solution.py:642

commit v4 on v3

--- a/solution.py
+++ b/solution.py
@@ -163,7 +163,7 @@
 
 def kernel(
     src_hbm, init_hbm, abs_hbm, out_ref,
-    src, ab, init, tbuf, sbuf, spec, kc, uu, ee, epart, ends, before, dext, va, vb, kk, join, f1, obuf,
+    src, ab, init, tbuf, sbuf, spec, kc, uu, ee, epart, ends, before, dext, va, vb, kk, join, back, f1, obuf,
     lsem, t1s, t1r, t2s, t2r, rss, rsr, wns, wnr, has, har, t3s, t3r, t4s, t4r,
 ):
     s = lax.axis_index("step")
@@ -361,16 +361,27 @@
 
     @pl.when(active)
     def _():
+        def begin(dx, dy, count):
+            rows = pl.ds(dy, B)
+            for m in range(count):
+                k1, k2, kb = (kc[n, dx + m, rows, :] for n in range(3))
+                s0, s1 = (spec[n, dx + m, rows, :] for n in range(2))
+                inner = pl.ds(pl.multiple_of(dy + 8, 8), B)
+                uu[0, 0, dx + m + 1, inner, :] = k1 * s0 - kb * s1
+                uu[0, 1, dx + m + 1, inner, :] = k2 * s1 + kb * s0
+
         for c in range(2):
             spec[c, pl.ds(x0, B), pl.ds(y0, B), :] = sbuf[slot, c]
-        for shift in reversed(OFFSETS):
-            d = device(shift)
-            dx, dy = origin(d)
-            for h in range(PARTS):
+        begin(x0, y0, B)
+        for h in range(PARTS):
+            for shift in reversed(EVEN + ODD):
+                d = device(shift)
+                dx, dy = origin(d)
                 remote(
                     sbuf.at[slot, :, pl.ds(0, PB)], spec.at[:, pl.ds(dx + h * PB, PB), pl.ds(dy, B)],
                     t2s.at[0, h], t2r.at[d, h], step=d,
                 ).wait_recv()
+                begin(dx + h * PB, dy, PB)
 
     lane = lax.broadcasted_iota(jnp.int32, (8, NZ), 1)
 
@@ -381,35 +392,24 @@
         above = jnp.where(at == NZ - 1, 0.0, pltpu.roll(v, NZ - 1, 1))
         return below + above
 
-    def neighbours(load, x, y, n):
-        total = load(x - 1, y, n) + load(x + 1, y, n)
-        total = total + (load(x, y - 1, n) + load(x, y + 1, n))
-        return total + z_sum(load(x, y, n))
-
     p_end = 2.0 / (16 * GAMMA**15)
     ends_re = table([0.5 * p_end] + [p_end * v for v in cos_of[1:]], slot)
     ends_im = table([-0.5 * p_end] + [p_end * v for v in sin_of[1:]], slot)
 
     @pl.when(active)
     def _():
-        def start(x, c):
-            k1, k2, kb = (kc[n, x, pl.ds(0, NY), :] for n in range(3))
-            s0, s1 = (spec[n, x, pl.ds(0, NY), :] for n in range(2))
-            uu[0, 0, x + 1, pl.ds(8, NY), :] = k1 * s0 - kb * s1
-            uu[0, 1, x + 1, pl.ds(8, NY), :] = k2 * s1 + kb * s0
-            return c
-
-        lax.fori_loop(0, NX, start, 0, unroll=4)
-
         def sweep(k, c):
             old = k % 2
+
+            def load(q, px, py):
+                return uu[old, q, px, pl.ds(py, NY), :]
+
             for x in range(NX):
-                nb = [
-                    neighbours(
-                        lambda px, py, n, q=q: uu[old, q, px, pl.ds(py, n), :], x + 1, 8, NY
-                    )
-                    for q in range(2)
-                ]
+                nb = []
+                for q in range(2):
+                    t = load(q, x, 8) + load(q, x + 2, 8)
+                    t = t + (load(q, x + 1, 7) + load(q, x + 1, 9))
+                    nb.append(t + z_sum(load(q, x + 1, 8)))
                 k1, k2, kb = (kc[n, x, pl.ds(0, NY), :] for n in range(3))
                 s0, s1 = (spec[n, x, pl.ds(0, NY), :] + nb[n] for n in range(2))
                 uu[1 - old, 0, x + 1, pl.ds(8, NY), :] = k1 * s0 - kb * s1
@@ -449,6 +449,25 @@
 
     to_next = remote(ends, before, wns.at[0], wnr.at[0], win=(w + 1) % WINDOWS)
     to_next.start()
+    def from_slot(k, h, shift):
+        d = device(shift)
+        dx, dy = origin(d)
+        return remote(
+            uu.at[1, :, pl.ds(dx + h * PB + 1, PB), pl.ds(pl.multiple_of(dy + 8, 8), B)],
+            f1.at[slot, :, pl.ds(h * PB, PB)], t3s.at[k, h], t3r.at[slot, h], step=d,
+        )
+
+    def return_field(h):
+        @pl.when(active)
+        def _():
+            for k, shift in enumerate(OFFSETS):
+                from_slot(k, h, shift).start()
+            for c in range(2):
+                f1[slot, c, pl.ds(h * PB, PB)] = uu[
+                    1, c, pl.ds(x0 + h * PB + 1, PB), pl.ds(pl.multiple_of(y0 + 8, 8), B), :
+                ]
+
+    return_field(0)
     to_next.wait_recv()
     later_window = jnp.where(w == 0, jnp.float32(0.0), jnp.float32(1.0 / COUPLING))
     change = later_window * before[...] - (ALPHA / COUPLING) * ends[...]
@@ -457,7 +476,7 @@
     ).astype(BF16)
     dext[pl.ds(B, B), pl.ds(B, B), :] = spread(change.reshape(B * B, NZ), pack).reshape(B, B, NZ)
 
-    shifts = [(i, j) for i in (-1, 0, 1) for j in (-1, 0, 1) if (i, j) != (0, 0)]
+    shifts = [(0, 1), (0, -1), (1, 0), (-1, 0), (1, 1), (-1, -1), (1, -1), (-1, 1)]
     centre = dext.at[pl.ds(B, B), pl.ds(B, B)]
     halo = []
     for k, (i, j) in enumerate(shifts):
@@ -468,39 +487,31 @@
         copy.start()
         halo.append(copy)
 
-    for copy in halo:
-        copy.wait_recv()
-
-    @pl.when(active)
-    def _():
-        for k, shift in enumerate(OFFSETS):
-            d = device(shift)
-            dx, dy = origin(d)
-            remote(
-                uu.at[1, :, pl.ds(dx + 1, B), pl.ds(pl.multiple_of(dy + 8, 8), B)],
-                f1.at[slot], t3s.at[k], t3r.at[slot], step=d,
-            ).start()
-        for c in range(2):
-            f1[slot, c] = uu[1, c, pl.ds(x0 + 1, B), pl.ds(pl.multiple_of(y0 + 8, 8), B), :]
-
-
-    def wide_start(i, c):
-        rows = pl.ds(pl.multiple_of(i * PITCH, PITCH), 3 * B)
-        v = dext[i, pl.ds(0, 3 * B), :]
-        swapped = pltpu.roll(v, HALF, 1)
-        d = [jnp.where(low, v, swapped), jnp.where(low, swapped, v)]
-        for odd in range(2):
-            kk[dd(odd), rows, :] = d[odd]
-            kk[dz(odd), rows, :] = jnp.where(low, d[odd], 0.0)
-            for p in range(PAIRS):
-                second = kk[part(p, odd, 1), rows, :]
-                if p == 0:
-                    second = jnp.where(low, kk[kz(odd), rows, :], second)
-                va[part(p, odd, 0), rows, :] = kk[part(p, odd, 0), rows, :] * d[odd]
-                va[part(p, odd, 1), rows, :] = second * d[odd]
-        return c
-
-    lax.fori_loop(1, 3 * B - 1, wide_start, 0)
+    def wide_start(i, j):
+        row = B - B * j
+        mask = low[:B]
+        for plane in range(max(B - B * i, 1), min(2 * B - B * i, 3 * B - 1)):
+            rows = pl.ds(plane * PITCH + row, B)
+            v = dext[plane, pl.ds(row, B), :]
+            swapped = pltpu.roll(v, HALF, 1)
+            d = [jnp.where(mask, v, swapped), jnp.where(mask, swapped, v)]
+            for odd in range(2):
+                kk[dd(odd), rows, :] = d[odd]
+                kk[dz(odd), rows, :] = jnp.where(mask, d[odd], 0.0)
+                for p in range(PAIRS):
+                    second = kk[part(p, odd, 1), rows, :]
+                    if p == 0:
+                        second = jnp.where(mask, kk[kz(odd), rows, :], second)
+                    va[part(p, odd, 0), rows, :] = kk[part(p, odd, 0), rows, :] * d[odd]
+                    va[part(p, odd, 1), rows, :] = second * d[odd]
+
+    wide_start(0, 0)
+    for k, (i, j) in enumerate(shifts):
+        halo[k].wait_recv()
+        wide_start(i, j)
+
+    return_field(1)
+
     zero_row = s // STEPS
     for k in range(SWEEPS - 1):
         reach = SWEEPS - 2 - k
@@ -535,40 +546,60 @@
 
         lax.fori_loop(0, 2, wide, 0)
 
-    slots_wait(
-        lambda f, d: remote(uu.at[1, :, pl.ds(0, B), pl.ds(0, B)], f1.at[f], t3s.at[0], t3r.at[f], step=d).wait_recv()
-    )
-
-    for p in range(PAIRS):
-        for q in range(2):
-            mixed = jnp.concatenate(
-                [
-                    jnp.concatenate([vb[part(p, odd, q), pl.ds((B + x) * PITCH + B, B), :] for x in range(B)], 0)
+    def natural(h):
+        mixed = []
+        for p in range(PAIRS):
+            for q in range(2):
+                sides = [
+                    jnp.concatenate(
+                        [vb[part(p, odd, q), pl.ds((B + h * PB + x) * PITCH + B, B), :] for x in range(PB)], 0
+                    )
                     for odd in range(2)
-                ],
-                1,
-            )
-            natural = spread(mixed, join[...], 2)
-            for h in range(2):
-                f = p + h * PAIRS
-                f1[f, q] = f1[f, q] + natural[:, h * NZ : (h + 1) * NZ].reshape(B, B, NZ)
-
-    def untransform(x, c):
-        total = [[f1[f, q, x] for q in range(2)] for f in range(SLOTS)]
-        spectrum = [(total[0][0], None)] + [tuple(v) for v in total[1:]] + [(total[0][1], None)]
-        values = irdft(spectrum, STEPS)
-        for t in range(STEPS):
-            obuf[t, x] = values[t]
-        return c
-
-    lax.fori_loop(0, B, untransform, 0)
-    t4 = []
-    for k, shift in enumerate(OFFSETS):
+                ]
+                mixed.append(jnp.concatenate(sides, 1))
+        mixed = jnp.concatenate(mixed, 0)
+        high = mixed.astype(BF16)
+        rest = (mixed - high.astype(F32)).astype(BF16)
+        n = mixed.shape[0]
+        both = jnp.dot(jnp.concatenate([high, rest], 0), join[...], preferred_element_type=F32)
+        back[...] = both[:n] + both[n:]
+
+    def untransform(h):
+        for x in range(PB):
+            total = []
+            for f in range(SLOTS):
+                lanes = pl.ds(f // PAIRS * NZ, NZ)
+                total.append(
+                    [
+                        f1[f, q, h * PB + x]
+                        + back[pl.ds(((f % PAIRS * 2 + q) * PB + x) * B, B), lanes]
+                        for q in range(2)
+                    ]
+                )
+            spectrum = [(total[0][0], None)] + [tuple(v) for v in total[1:]] + [(total[0][1], None)]
+            values = irdft(spectrum, STEPS)
+            for t in range(STEPS):
+                obuf[t, h * PB + x] = values[t]
+
+    def to_step(k, h, shift):
         d = device(shift)
-        copy = remote(obuf.at[d], out_ref.at[pl.ds(x0, B), pl.ds(y0, B)], t4s.at[k], t4r.at[s], step=d)
-        copy.start()
-        t4.append(copy)
-    out_ref[pl.ds(x0, B), pl.ds(y0, B), :] = obuf[s]
+        return remote(
+            obuf.at[d, pl.ds(h * PB, PB)], out_ref.at[pl.ds(x0 + h * PB, PB), pl.ds(y0, B)],
+            t4s.at[k, h], t4r.at[s, h], step=d,
+        )
+
+    for h in range(PARTS):
+        natural(h)
+        slots_wait(
+            lambda f, d: remote(
+                uu.at[1, :, pl.ds(0, PB), pl.ds(0, B)], f1.at[f, :, pl.ds(h * PB, PB)],
+                t3s.at[0, h], t3r.at[f, h], step=d,
+            ).wait_recv()
+        )
+        untransform(h)
+        for k, shift in enumerate(OFFSETS):
+            to_step(k, h, shift).start()
+        out_ref[pl.ds(x0 + h * PB, PB), pl.ds(y0, B), :] = obuf[s, pl.ds(h * PB, PB)]
 
     for copy in t1:
         copy.wait_send()
@@ -583,16 +614,19 @@
         for k, shift in enumerate(OFFSETS):
             d = device(shift)
             remote(ee.at[block], epart.at[slot], rss.at[k], rsr.at[slot], step=d).wait_send()
+            for h in range(PARTS):
+                from_slot(k, h, shift).wait_send()
+
+    for h in range(PARTS):
+        for k in range(1, STEPS):
+            d = (s + k) % STEPS
+            dx, dy = origin(d)
             remote(
-                uu.at[1, :, pl.ds(0, B), pl.ds(0, B)], f1.at[slot], t3s.at[k], t3r.at[slot], step=d
-            ).wait_send()
-
-    for k in range(1, STEPS):
-        d = (s + k) % STEPS
-        dx, dy = origin(d)
-        remote(obuf.at[d], out_ref.at[pl.ds(dx, B), pl.ds(dy, B)], t4s.at[k], t4r.at[d], step=d).wait_recv()
-    for copy in t4:
-        copy.wait_send()
+                obuf.at[d, pl.ds(0, PB)], out_ref.at[pl.ds(dx + h * PB, PB), pl.ds(dy, B)],
+                t4s.at[0, h], t4r.at[d, h], step=d,
+            ).wait_recv()
+        for k, shift in enumerate(OFFSETS):
+            to_step(k, h, shift).wait_send()
 
 
 def per_device(initial_state, source, absorption):
@@ -622,6 +656,7 @@
             vmem(16, 3 * B * PITCH + 8, NZ),
             vmem(28, 3 * B * PITCH + 8, NZ),
             pltpu.VMEM((2 * NZ, 2 * NZ), BF16),
+            vmem(2 * PAIRS * PB * B, 2 * NZ),
             vmem(SLOTS, 2, B, B, NZ),
             vmem(STEPS, B, B, NZ),
             dma(3),
@@ -630,8 +665,8 @@
             dma(STEPS), dma(SLOTS),
             dma(1), dma(1),
             dma(8), dma(8),
-            dma(STEPS), dma(SLOTS),
-            dma(STEPS), dma(STEPS),
+            dma(STEPS, PARTS), dma(SLOTS, PARTS),
+            dma(STEPS, PARTS), dma(STEPS, PARTS),
         ],
         compiler_params=pltpu.CompilerParams(
             collective_id=0, has_side_effects=True, vmem_limit_bytes=60 * 2**20

time: 57.7 us -> 57.1 us (0.990)
  no operation moved by 1% of the time
where the time goes in v4:
time: 57.1 us; the launch traced here: 57 us
  Pallas kernels  56.1 us (98%)
  other arithmetic  0.84 us (1%)
    pallas_call x1, Pallas kernels, per_device(): pl.pallas_call(kernel, out_shape=pltpu.VMEM(grid, F32), in_specs=[pl.Bloc...  56.1 us

profile of v4, /device:TPU:0, one launch (start us, length us, event | category | flops | bytes accessed | tf_op | source)
XLA Modules:
  0.0 57.0 jit_solution(5095148293533047220)
XLA Ops:
  0.0 56.1 %windows.1 = f32[32,32,128]{2,1,0:T(8,128)S(1)} custom-call(f32[32,32,128]{2,1,0:T(8,128)} %bitcast.3, f32[32,32,128]{2,1,0:T(8,128)} %init_hbm.1, f32[32,32,128]{2,1,0:T(8,128)} %abs_hbm.1), custom_call_target="tpu_custom_call" | custom-call | tf_op jit(solution)/shard_map/windows/pallas_call | solution.py:636
  56.1 0.8 %multiply_bitcast_fusion = f32[1,1,32,32,128]{4,3,2,1,0:T(8,128)} fusion(f32[32,32,128]{2,1,0:T(8,128)S(1)} %windows.1, f32[]{:T(128)S(6)} %div.3), kind=kLoop, calls=%fused_computation | loop fusion | flops 131072 | bytes 1048580 | tf_op jit(solution)/shard_map/broadcast_in_dim | solution.py:677

commit v5 on v4

--- a/solution.py
+++ b/solution.py
@@ -35,6 +35,8 @@
 ODD = [d for d in OFFSETS if sum(d) % 2 == 1]
 PARTS = 2
 PB = B // PARTS
+PIECES = 2
+PC = B // PIECES
 
 
 def wpow(n, k):
@@ -191,6 +193,10 @@
     def device(shift):
         return (bx + shift[0]) % 4 * 4 + (by + shift[1]) % 4
 
+    def counted(messages, rows, send, recv):
+        size = va.at[pl.ds(0, messages), pl.ds(0, rows)]
+        return remote(size, size, send, recv, step=(s + 1) % STEPS)
+
     load_src = pltpu.make_async_copy(src_hbm, src, lsem.at[0])
     load_abs = pltpu.make_async_copy(abs_hbm, ab, lsem.at[1])
     load_init = pltpu.make_async_copy(init_hbm.at[pl.ds(x0, B), pl.ds(y0, B)], init, lsem.at[2])
@@ -206,17 +212,15 @@
     pl.semaphore_wait(barrier, STEPS - 1 + 2)
     load_src.wait()
 
-    t1 = []
-    for h in range(PARTS):
+    for h in range(PIECES):
         for k, shift in enumerate(OFFSETS):
             d = device(shift)
             dx, dy = origin(d)
             copy = remote(
-                src.at[pl.ds(dx + h * PB, PB), pl.ds(dy, B)], tbuf.at[s, pl.ds(h * PB, PB)],
-                t1s.at[k, h], t1r.at[s, h], step=d,
+                src.at[pl.ds(dx + h * PC, PC), pl.ds(dy, B)], tbuf.at[s, pl.ds(h * PC, PC)],
+                t1s.at[0], t1r.at[h], step=d,
             )
             copy.start()
-            t1.append(copy)
     load_init.wait()
     load_abs.wait()
     tbuf[s] = src[pl.ds(x0, B), pl.ds(y0, B), :]
@@ -278,34 +282,27 @@
 
     def to_slot(k, h, shift):
         d = device(shift)
-        half = pl.ds(x0 + h * PB, PB)
+        half = pl.ds(x0 + h * PC, PC)
         return remote(
-            sbuf.at[d // 2, :, pl.ds(h * PB, PB)], spec.at[:, half, pl.ds(y0, B)],
-            t2s.at[k, h], t2r.at[s, h], step=d,
+            sbuf.at[d // 2, :, pl.ds(h * PC, PC)], spec.at[:, half, pl.ds(y0, B)],
+            t2s.at[0], t2r.at[h], step=d,
         )
 
-    def send_to_slots(act):
-        def run(h):
-            @pl.when(active)
-            def _():
-                for k, shift in enumerate(EVEN):
-                    act(to_slot(k, h, shift))
-
-            @pl.when(jnp.logical_not(active))
-            def _():
-                for k, shift in enumerate(ODD):
-                    act(to_slot(k, h, shift))
-
-        return run
-
-    for h in range(PARTS):
-        for k in range(1, STEPS):
-            d = (s - k) % STEPS
-            remote(
-                src.at[pl.ds(0, PB), pl.ds(0, B)], tbuf.at[d, pl.ds(h * PB, PB)], t1s.at[0, h], t1r.at[d, h], step=d
-            ).wait_recv()
-        lax.fori_loop(h * PB, (h + 1) * PB, transform, 0)
-        send_to_slots(lambda copy: copy.start())(h)
+    def send_to_slots(h):
+        @pl.when(active)
+        def _():
+            for k, shift in enumerate(EVEN):
+                to_slot(k, h, shift).start()
+
+        @pl.when(jnp.logical_not(active))
+        def _():
+            for k, shift in enumerate(ODD):
+                to_slot(k, h, shift).start()
+
+    for h in range(PIECES):
+        counted(STEPS - 1, PC * B, t1s.at[0], t1r.at[h]).wait_recv()
+        lax.fori_loop(h * PC, (h + 1) * PC, transform, 0)
+        send_to_slots(h)
 
     wide_lane = lax.broadcasted_iota(jnp.int32, (3 * B, NZ), 1)
     low = wide_lane < HALF
@@ -361,27 +358,21 @@
 
     @pl.when(active)
     def _():
-        def begin(dx, dy, count):
-            rows = pl.ds(dy, B)
-            for m in range(count):
-                k1, k2, kb = (kc[n, dx + m, rows, :] for n in range(3))
-                s0, s1 = (spec[n, dx + m, rows, :] for n in range(2))
-                inner = pl.ds(pl.multiple_of(dy + 8, 8), B)
-                uu[0, 0, dx + m + 1, inner, :] = k1 * s0 - kb * s1
-                uu[0, 1, dx + m + 1, inner, :] = k2 * s1 + kb * s0
-
         for c in range(2):
             spec[c, pl.ds(x0, B), pl.ds(y0, B), :] = sbuf[slot, c]
-        begin(x0, y0, B)
-        for h in range(PARTS):
-            for shift in reversed(EVEN + ODD):
-                d = device(shift)
-                dx, dy = origin(d)
-                remote(
-                    sbuf.at[slot, :, pl.ds(0, PB)], spec.at[:, pl.ds(dx + h * PB, PB), pl.ds(dy, B)],
-                    t2s.at[0, h], t2r.at[d, h], step=d,
-                ).wait_recv()
-                begin(dx + h * PB, dy, PB)
+        for h in range(PIECES):
+            counted(STEPS - 1, 2 * PC * B, t2s.at[0], t2r.at[h]).wait_recv()
+
+            def begin(i, c, h=h):
+                for m in range(PC):
+                    x = i * B + h * PC + m
+                    k1, k2, kb = (kc[n, x, pl.ds(0, NY), :] for n in range(3))
+                    s0, s1 = (spec[n, x, pl.ds(0, NY), :] for n in range(2))
+                    uu[0, 0, x + 1, pl.ds(8, NY), :] = k1 * s0 - kb * s1
+                    uu[0, 1, x + 1, pl.ds(8, NY), :] = k2 * s1 + kb * s0
+                return c
+
+            lax.fori_loop(0, NX // B, begin, 0)
 
     lane = lax.broadcasted_iota(jnp.int32, (8, NZ), 1)
 
@@ -428,19 +419,14 @@
         for k, shift in enumerate(OFFSETS):
             d = device(shift)
             dx, dy = origin(d)
-            remote(ee.at[pl.ds(dx, B), pl.ds(dy, B)], epart.at[slot], rss.at[k], rsr.at[slot], step=d).start()
+            remote(ee.at[pl.ds(dx, B), pl.ds(dy, B)], epart.at[slot], rss.at[0], rsr.at[0], step=d).start()
         epart[slot] = ee[pl.ds(x0, B), pl.ds(y0, B), :]
 
-    partner = s + 1 - 2 * (s % 2)
-
-    def slots_wait(wait):
-        for k in range(1, SLOTS):
-            f = (slot + k) % SLOTS
-            wait(f, slot_device(f))
-        pl.when(jnp.logical_not(active))(lambda: wait(slot, partner))
-
-    block = (pl.ds(0, B), pl.ds(0, B))
-    slots_wait(lambda f, d: remote(ee.at[block], epart.at[f], rss.at[0], rsr.at[f], step=d).wait_recv())
+    def slots_wait(rows, send, recv):
+        pl.when(active)(lambda: counted(SLOTS - 1, rows, send, recv).wait_recv())
+        pl.when(jnp.logical_not(active))(lambda: counted(SLOTS, rows, send, recv).wait_recv())
+
+    slots_wait(B * B, rss.at[0], rsr.at[0])
     for x in range(B):
         total = epart[0, x]
         for f in range(1, SLOTS):
@@ -454,7 +440,7 @@
         dx, dy = origin(d)
         return remote(
             uu.at[1, :, pl.ds(dx + h * PB + 1, PB), pl.ds(pl.multiple_of(dy + 8, 8), B)],
-            f1.at[slot, :, pl.ds(h * PB, PB)], t3s.at[k, h], t3r.at[slot, h], step=d,
+            f1.at[slot, :, pl.ds(h * PB, PB)], t3s.at[0], t3r.at[h], step=d,
         )
 
     def return_field(h):
@@ -477,20 +463,22 @@
     dext[pl.ds(B, B), pl.ds(B, B), :] = spread(change.reshape(B * B, NZ), pack).reshape(B, B, NZ)
 
     shifts = [(0, 1), (0, -1), (1, 0), (-1, 0), (1, 1), (-1, -1), (1, -1), (-1, 1)]
-    centre = dext.at[pl.ds(B, B), pl.ds(B, B)]
-    halo = []
     for k, (i, j) in enumerate(shifts):
         d = ((bx + i + 4) % 4) * 4 + (by + j + 4) % 4
-        copy = remote(
-            centre, dext.at[pl.ds(B - B * i, B), pl.ds(B - B * j, B)], has.at[k], har.at[k], step=d
-        )
-        copy.start()
-        halo.append(copy)
+        n = B - abs(i) * (1 + abs(j))
+        first = B if i < 1 else 2 * B - n
+        remote(
+            dext.at[pl.ds(first, n), pl.ds(B, B)],
+            dext.at[pl.ds(first - B * i, n), pl.ds(B - B * j, B)],
+            has.at[0], har.at[k // 4], step=d,
+        ).start()
 
     def wide_start(i, j):
         row = B - B * j
         mask = low[:B]
-        for plane in range(max(B - B * i, 1), min(2 * B - B * i, 3 * B - 1)):
+        n = B - abs(i) * (1 + abs(j))
+        first = (B if i < 1 else 2 * B - n) - B * i
+        for plane in range(first, first + n):
             rows = pl.ds(plane * PITCH + row, B)
             v = dext[plane, pl.ds(row, B), :]
             swapped = pltpu.roll(v, HALF, 1)
@@ -506,9 +494,10 @@
                     va[part(p, odd, 1), rows, :] = second * d[odd]
 
     wide_start(0, 0)
-    for k, (i, j) in enumerate(shifts):
-        halo[k].wait_recv()
-        wide_start(i, j)
+    for k in range(2):
+        counted(4, (60, 48)[k], has.at[0], har.at[k]).wait_recv()
+        for i, j in shifts[4 * k : 4 * k + 4]:
+            wide_start(i, j)
 
     return_field(1)
 
@@ -585,48 +574,34 @@
         d = device(shift)
         return remote(
             obuf.at[d, pl.ds(h * PB, PB)], out_ref.at[pl.ds(x0 + h * PB, PB), pl.ds(y0, B)],
-            t4s.at[k, h], t4r.at[s, h], step=d,
+            t4s.at[0], t4r.at[0], step=d,
         )
 
     for h in range(PARTS):
         natural(h)
-        slots_wait(
-            lambda f, d: remote(
-                uu.at[1, :, pl.ds(0, PB), pl.ds(0, B)], f1.at[f, :, pl.ds(h * PB, PB)],
-                t3s.at[0, h], t3r.at[f, h], step=d,
-            ).wait_recv()
-        )
+        slots_wait(2 * PB * B, t3s.at[0], t3r.at[h])
         untransform(h)
         for k, shift in enumerate(OFFSETS):
             to_step(k, h, shift).start()
         out_ref[pl.ds(x0 + h * PB, PB), pl.ds(y0, B), :] = obuf[s, pl.ds(h * PB, PB)]
 
-    for copy in t1:
-        copy.wait_send()
-    for h in range(PARTS):
-        send_to_slots(lambda copy: copy.wait_send())(h)
+    counted(STEPS - 1, B * B, t1s.at[0], t1r.at[0]).wait_send()
     to_next.wait_send()
-    for copy in halo:
-        copy.wait_send()
+    counted(8, 54, has.at[0], har.at[0]).wait_send()
 
     @pl.when(active)
     def _():
-        for k, shift in enumerate(OFFSETS):
-            d = device(shift)
-            remote(ee.at[block], epart.at[slot], rss.at[k], rsr.at[slot], step=d).wait_send()
-            for h in range(PARTS):
-                from_slot(k, h, shift).wait_send()
-
-    for h in range(PARTS):
-        for k in range(1, STEPS):
-            d = (s + k) % STEPS
-            dx, dy = origin(d)
-            remote(
-                obuf.at[d, pl.ds(0, PB)], out_ref.at[pl.ds(dx + h * PB, PB), pl.ds(dy, B)],
-                t4s.at[0, h], t4r.at[d, h], step=d,
-            ).wait_recv()
-        for k, shift in enumerate(OFFSETS):
-            to_step(k, h, shift).wait_send()
+        counted(SLOTS - 1, 2 * B * B, t2s.at[0], t2r.at[0]).wait_send()
+        counted(STEPS - 1, B * B, rss.at[0], rsr.at[0]).wait_send()
+        counted(STEPS - 1, 2 * B * B, t3s.at[0], t3r.at[0]).wait_send()
+
+    @pl.when(jnp.logical_not(active))
+    def _():
+        counted(SLOTS, 2 * B * B, t2s.at[0], t2r.at[0]).wait_send()
+
+    last = counted(STEPS - 1, B * B, t4s.at[0], t4r.at[0])
+    last.wait_send()
+    last.wait_recv()
 
 
 def per_device(initial_state, source, absorption):
@@ -660,13 +635,13 @@
             vmem(SLOTS, 2, B, B, NZ),
             vmem(STEPS, B, B, NZ),
             dma(3),
-            dma(STEPS, PARTS), dma(STEPS, PARTS),
-            dma(SLOTS, PARTS), dma(STEPS, PARTS),
-            dma(STEPS), dma(SLOTS),
+            dma(1), dma(PIECES),
+            dma(1), dma(PIECES),
             dma(1), dma(1),
-            dma(8), dma(8),
-            dma(STEPS, PARTS), dma(SLOTS, PARTS),
-            dma(STEPS, PARTS), dma(STEPS, PARTS),
+            dma(1), dma(1),
+            dma(1), dma(2),
+            dma(1), dma(PARTS),
+            dma(1), dma(1),
         ],
         compiler_params=pltpu.CompilerParams(
             collective_id=0, has_side_effects=True, vmem_limit_bytes=60 * 2**20

time: 57.1 us -> 54.3 us (0.951)
  Pallas kernels: 56.1 us -> 53.3 us
    pallas_call x1, Pallas kernels: 56.1 us -> 53.3 us  [per_device(): pl.pallas_call(kernel, out_shape=pltpu.VMEM(grid, F32), in_specs=[pl.Bloc...]
where the time goes in v5:
time: 54.3 us; the launch traced here: 54.2 us
  Pallas kernels  53.3 us (98%)
  other arithmetic  0.84 us (2%)
    pallas_call x1, Pallas kernels, per_device(): pl.pallas_call(kernel, out_shape=pltpu.VMEM(grid, F32), in_specs=[pl.Bloc...  53.3 us

profile of v5, /device:TPU:0, one launch (start us, length us, event | category | flops | bytes accessed | tf_op | source)
XLA Modules:
  0.0 54.2 jit_solution(5280529684422683887)
XLA Ops:
  0.0 53.3 %windows.1 = f32[32,32,128]{2,1,0:T(8,128)S(1)} custom-call(f32[32,32,128]{2,1,0:T(8,128)} %bitcast.3, f32[32,32,128]{2,1,0:T(8,128)} %init_hbm.1, f32[32,32,128]{2,1,0:T(8,128)} %abs_hbm.1), custom_call_target="tpu_custom_call" | custom-call | tf_op jit(solution)/shard_map/windows/pallas_call | solution.py:611
  53.4 0.8 %multiply_bitcast_fusion = f32[1,1,32,32,128]{4,3,2,1,0:T(8,128)} fusion(f32[32,32,128]{2,1,0:T(8,128)S(1)} %windows.1, f32[]{:T(128)S(6)} %div.3), kind=kLoop, calls=%fused_computation | loop fusion | flops 131072 | bytes 1048580 | tf_op jit(solution)/shard_map/broadcast_in_dim | solution.py:652

commit v6 on v5

--- a/solution.py
+++ b/solution.py
@@ -422,19 +422,6 @@
             remote(ee.at[pl.ds(dx, B), pl.ds(dy, B)], epart.at[slot], rss.at[0], rsr.at[0], step=d).start()
         epart[slot] = ee[pl.ds(x0, B), pl.ds(y0, B), :]
 
-    def slots_wait(rows, send, recv):
-        pl.when(active)(lambda: counted(SLOTS - 1, rows, send, recv).wait_recv())
-        pl.when(jnp.logical_not(active))(lambda: counted(SLOTS, rows, send, recv).wait_recv())
-
-    slots_wait(B * B, rss.at[0], rsr.at[0])
-    for x in range(B):
-        total = epart[0, x]
-        for f in range(1, SLOTS):
-            total = total + epart[f, x]
-        ends[x] = total
-
-    to_next = remote(ends, before, wns.at[0], wnr.at[0], win=(w + 1) % WINDOWS)
-    to_next.start()
     def from_slot(k, h, shift):
         d = device(shift)
         dx, dy = origin(d)
@@ -454,6 +441,20 @@
                 ]
 
     return_field(0)
+
+    def slots_wait(rows, send, recv):
+        pl.when(active)(lambda: counted(SLOTS - 1, rows, send, recv).wait_recv())
+        pl.when(jnp.logical_not(active))(lambda: counted(SLOTS, rows, send, recv).wait_recv())
+
+    slots_wait(B * B, rss.at[0], rsr.at[0])
+    for x in range(B):
+        total = epart[0, x]
+        for f in range(1, SLOTS):
+            total = total + epart[f, x]
+        ends[x] = total
+
+    to_next = remote(ends, before, wns.at[0], wnr.at[0], win=(w + 1) % WINDOWS)
+    to_next.start()
     to_next.wait_recv()
     later_window = jnp.where(w == 0, jnp.float32(0.0), jnp.float32(1.0 / COUPLING))
     change = later_window * before[...] - (ALPHA / COUPLING) * ends[...]

time: 54.3 us -> 53.3 us (0.982)
  Pallas kernels: 53.3 us -> 52.3 us
    pallas_call x1, Pallas kernels: 53.3 us -> 52.3 us  [per_device(): pl.pallas_call(kernel, out_shape=pltpu.VMEM(grid, F32), in_specs=[pl.Bloc...]
where the time goes in v6:
time: 53.3 us; the launch traced here: 53.2 us
  Pallas kernels  52.3 us (98%)
  other arithmetic  0.84 us (2%)
    pallas_call x1, Pallas kernels, per_device(): pl.pallas_call(kernel, out_shape=pltpu.VMEM(grid, F32), in_specs=[pl.Bloc...  52.3 us

profile of v6, /device:TPU:0, one launch (start us, length us, event | category | flops | bytes accessed | tf_op | source)
XLA Modules:
  0.0 53.2 jit_solution(2225522444854995756)
XLA Ops:
  0.0 52.3 %windows.1 = f32[32,32,128]{2,1,0:T(8,128)S(1)} custom-call(f32[32,32,128]{2,1,0:T(8,128)} %bitcast.3, f32[32,32,128]{2,1,0:T(8,128)} %init_hbm.1, f32[32,32,128]{2,1,0:T(8,128)} %abs_hbm.1), custom_call_target="tpu_custom_call" | custom-call | tf_op jit(solution)/shard_map/windows/pallas_call | solution.py:612
  52.4 0.8 %multiply_bitcast_fusion = f32[1,1,32,32,128]{4,3,2,1,0:T(8,128)} fusion(f32[32,32,128]{2,1,0:T(8,128)S(1)} %windows.1, f32[]{:T(128)S(6)} %div.3), kind=kLoop, calls=%fused_computation | loop fusion | flops 131072 | bytes 1048580 | tf_op jit(solution)/shard_map/broadcast_in_dim | solution.py:653

commit v7 on v6

--- a/solution.py
+++ b/solution.py
@@ -37,6 +37,8 @@
 PB = B // PARTS
 PIECES = 2
 PC = B // PIECES
+TURNS = 4
+PT = B // TURNS
 
 
 def wpow(n, k):
@@ -461,7 +463,7 @@
     pack = jnp.where(
         pick_z[:, :NZ] == 2 * (pick_l[:, :NZ] % HALF) + pick_l[:, :NZ] // HALF, 1.0, 0.0
     ).astype(BF16)
-    dext[pl.ds(B, B), pl.ds(B, B), :] = spread(change.reshape(B * B, NZ), pack).reshape(B, B, NZ)
+    dext[pl.ds(B, B), pl.ds(B, B), :] = spread(change.reshape(B * B, NZ), pack, 2).reshape(B, B, NZ)
 
     shifts = [(0, 1), (0, -1), (1, 0), (-1, 0), (1, 1), (-1, -1), (1, -1), (-1, 1)]
     for k, (i, j) in enumerate(shifts):
@@ -542,7 +544,7 @@
             for q in range(2):
                 sides = [
                     jnp.concatenate(
-                        [vb[part(p, odd, q), pl.ds((B + h * PB + x) * PITCH + B, B), :] for x in range(PB)], 0
+                        [vb[part(p, odd, q), pl.ds((B + h * PT + x) * PITCH + B, B), :] for x in range(PT)], 0
                     )
                     for odd in range(2)
                 ]
@@ -555,36 +557,37 @@
         back[...] = both[:n] + both[n:]
 
     def untransform(h):
-        for x in range(PB):
+        for x in range(PT):
             total = []
             for f in range(SLOTS):
                 lanes = pl.ds(f // PAIRS * NZ, NZ)
                 total.append(
                     [
-                        f1[f, q, h * PB + x]
-                        + back[pl.ds(((f % PAIRS * 2 + q) * PB + x) * B, B), lanes]
+                        f1[f, q, h * PT + x]
+                        + back[pl.ds(((f % PAIRS * 2 + q) * PT + x) * B, B), lanes]
                         for q in range(2)
                     ]
                 )
             spectrum = [(total[0][0], None)] + [tuple(v) for v in total[1:]] + [(total[0][1], None)]
             values = irdft(spectrum, STEPS)
             for t in range(STEPS):
-                obuf[t, h * PB + x] = values[t]
+                obuf[t, h * PT + x] = values[t]
 
     def to_step(k, h, shift):
         d = device(shift)
         return remote(
-            obuf.at[d, pl.ds(h * PB, PB)], out_ref.at[pl.ds(x0 + h * PB, PB), pl.ds(y0, B)],
+            obuf.at[d, pl.ds(h * PT, PT)], out_ref.at[pl.ds(x0 + h * PT, PT), pl.ds(y0, B)],
             t4s.at[0], t4r.at[0], step=d,
         )
 
-    for h in range(PARTS):
+    for h in range(TURNS):
         natural(h)
-        slots_wait(2 * PB * B, t3s.at[0], t3r.at[h])
+        if h % (TURNS // PARTS) == 0:
+            slots_wait(2 * PB * B, t3s.at[0], t3r.at[h // (TURNS // PARTS)])
         untransform(h)
         for k, shift in enumerate(OFFSETS):
             to_step(k, h, shift).start()
-        out_ref[pl.ds(x0 + h * PB, PB), pl.ds(y0, B), :] = obuf[s, pl.ds(h * PB, PB)]
+        out_ref[pl.ds(x0 + h * PT, PT), pl.ds(y0, B), :] = obuf[s, pl.ds(h * PT, PT)]
 
     counted(STEPS - 1, B * B, t1s.at[0], t1r.at[0]).wait_send()
     to_next.wait_send()
@@ -632,7 +635,7 @@
             vmem(16, 3 * B * PITCH + 8, NZ),
             vmem(28, 3 * B * PITCH + 8, NZ),
             pltpu.VMEM((2 * NZ, 2 * NZ), BF16),
-            vmem(2 * PAIRS * PB * B, 2 * NZ),
+            vmem(2 * PAIRS * PT * B, 2 * NZ),
             vmem(SLOTS, 2, B, B, NZ),
             vmem(STEPS, B, B, NZ),
             dma(3),
@@ -645,7 +648,7 @@
             dma(1), dma(1),
         ],
         compiler_params=pltpu.CompilerParams(
-            collective_id=0, has_side_effects=True, vmem_limit_bytes=60 * 2**20
+            collective_id=0, has_side_effects=True, vmem_limit_bytes=60 * 2**20,
         ),
         name="windows",
     )(source[0, 0], initial_state, absorption)

time: 53.3 us -> 53.6 us (level)
  no operation moved by 1% of the time
where the time goes in v7:
time: 53.6 us; the launch traced here: 53.5 us
  Pallas kernels  52.6 us (98%)
  other arithmetic  0.84 us (2%)
    pallas_call x1, Pallas kernels, per_device(): pl.pallas_call(kernel, out_shape=pltpu.VMEM(grid, F32), in_specs=[pl.Bloc...  52.6 us

profile of v7, /device:TPU:0, one launch (start us, length us, event | category | flops | bytes accessed | tf_op | source)
XLA Modules:
  0.0 53.5 jit_solution(13833265713580691398)
XLA Ops:
  0.0 52.6 %windows.1 = f32[32,32,128]{2,1,0:T(8,128)S(1)} custom-call(f32[32,32,128]{2,1,0:T(8,128)} %bitcast.3, f32[32,32,128]{2,1,0:T(8,128)} %init_hbm.1, f32[32,32,128]{2,1,0:T(8,128)} %abs_hbm.1), custom_call_target="tpu_custom_call" | custom-call | tf_op jit(solution)/shard_map/windows/pallas_call | solution.py:615
  52.6 0.8 %multiply_bitcast_fusion = f32[1,1,32,32,128]{4,3,2,1,0:T(8,128)} fusion(f32[32,32,128]{2,1,0:T(8,128)S(1)} %windows.1, f32[]{:T(128)S(6)} %div.3), kind=kLoop, calls=%fused_computation | loop fusion | flops 131072 | bytes 1048580 | tf_op jit(solution)/shard_map/broadcast_in_dim | solution.py:656
